TPU v7x, 256 devices: a whole 4x4x8 slice. The times are simulated.
256 devices in a mesh: layer: 2 (over core), ex: 128 (over z, y, x).
Axes of the slice: x: 4, y: 4, z: 8, core: 2. Of those that a mesh axis runs over, the one named last changes fastest.
Arguments:
- grads: bfloat16 [2, 32768, 512], P('layer', 'ex'), may hold values from -6 to 6
- labeled: int32 [32768], P('ex'), may hold values 0 or 1
- damping: float32 [2], P('layer'), may hold values from 0.05 to 0.5
Outputs:
- solved: float32 [2, 32768, 512], P('layer', 'ex')
- score: float32 [32768], P('ex')
All inputs are finite; a program needn't handle non-finite values. No bound on the sum of `labeled` on one device may be relied on, other than what follows from the above.
Results may differ from a plain program's by a relative error of at most 0.0003.
Values may be sent and summed in bfloat16 or wider, within the bound.
No kernel may reach another device: no remote copies, remote signals or barrier semaphores. Data moves between devices by JAX's collectives and lax.ppermute only.
A program may use at most 64 MiB of HBM per device.

v0:
```python
import jax
import jax.numpy as jnp
from jax import lax
from jax.sharding import Mesh
from jax.sharding import PartitionSpec as P

EX = ("ex_0", "ex_1", "ex_2")


def from_behind(value, axis, steps):
    count = lax.axis_size(axis)
    initial, last = (max(0, -steps), min(count, count - steps))
    return lax.ppermute(value, axis, [(source, source + steps) for source in range(initial, last)])


def rows_for(lines, devices):
    spare = -lines.shape[0] % devices
    if not spare:
        return lines
    return jnp.concatenate([lines, jnp.zeros((spare, *lines.shape[1:]), lines.dtype)])


def copy_for_each(array, axis):
    copies = jnp.broadcast_to(array, (lax.axis_size(axis), *array.shape))
    return lax.all_to_all(copies, axis, split_axis=0, concat_axis=0, tiled=True)


def joined_along(parts, dim):
    lengths = list(parts.shape[1:])
    lengths[dim] *= parts.shape[0]
    return jnp.moveaxis(parts, 0, dim).reshape(lengths)


def gathered_by_axis(array, axes, dim):
    far, near = axes
    parts = copy_for_each(copy_for_each(array, far), near)
    return joined_along(parts.swapaxes(0, 1).reshape(-1, *array.shape), dim)


def in_blocks(array, dim, devices):
    lengths = array.shape
    parts = array.reshape(*lengths[:dim], devices, lengths[dim] // devices, *lengths[dim + 1 :])
    return jnp.moveaxis(parts, dim, 0)


def sum_at_owner(array, axis, dim):
    parts = in_blocks(array, dim, lax.axis_size(axis))
    arrived = lax.all_to_all(parts, axis, split_axis=0, concat_axis=0, tiled=True)
    return arrived.sum(axis=0)


def summed_rows(array, axes, dim):
    far, near = axes
    own = sum_at_owner(in_blocks(array, dim, lax.axis_size(far)), near, dim + 1)
    return jnp.sum(lax.all_to_all(own, far, 0, 0, tiled=True), axis=0)


def sum_by_parts(array, axes):
    padded = rows_for(array, lax.axis_size(axes[0]) * lax.axis_size(axes[1]))
    whole = gathered_by_axis(summed_rows(padded, axes, 0), axes, 0)
    return lax.slice_in_dim(whole, 0, len(array)).reshape(array.shape)


def packed_total_2(arrays, axis):
    ravelled, at, gathered = (jnp.concatenate([a.reshape(-1) for a in arrays]), 0, [])
    subtotal = sum_by_parts(ravelled, axis)
    for a in arrays:
        gathered.append(subtotal[at : at + a.size].reshape(a.shape))
        at += a.size
    return tuple(gathered)


def total_of_pieces(array, axis):
    parts = lax.all_gather(array, axis)
    return parts.sum(axis=0)


def lower_solve(factor, right_hand):
    return jax.scipy.linalg.solve_triangular(factor, right_hand, lower=True)


def apply_inverse(factor, row_block):
    inner = jax.scipy.linalg.solve_triangular(factor, row_block.T, lower=True)
    return jax.scipy.linalg.solve_triangular(factor, inner, lower=True, trans=1).T


def pack_upper(blocks):
    layer_dev, sketch_width, unused_width = blocks.shape
    stripe_width = sketch_width // 8
    pieces = []
    for stripe in range(8):
        begin = stripe * stripe_width
        pieces.append(blocks[:, begin : begin + stripe_width, begin:].reshape(layer_dev, -1))
    return jnp.concatenate(pieces, 1)


def unpack_upper(packed_rows, sketch_width):
    layer_dev = packed_rows.shape[0]
    stripe_width = sketch_width // 8
    stripes = []
    offset = 0
    for stripe in range(8):
        begin = stripe * stripe_width
        span_size = stripe_width * (sketch_width - begin)
        piece = packed_rows[:, offset : offset + span_size].reshape(
            layer_dev, stripe_width, sketch_width - begin
        )
        stripes.append(jnp.pad(piece, ((0, 0), (0, 0), (begin, 0))))
        offset = offset + span_size
    upper = jnp.concatenate(stripes, 1)
    tile_index = jnp.arange(sketch_width, dtype=jnp.int32) // stripe_width
    keep_upper = (tile_index[:, None] <= tile_index[None, :])[None]
    return jnp.where(keep_upper, upper, jnp.swapaxes(upper, 1, 2))


def forward_layers(factor, trail, grads, diagonal, coupling):
    cross = lower_solve(factor, coupling[0])
    schur = diagonal[0] - jnp.dot(cross.T, cross, precision=lax.Precision.HIGHEST)
    left_side = grads[0].astype(jnp.float32) - jnp.dot(
        trail, coupling[0], precision=lax.Precision.HIGHEST
    )
    factor = jnp.linalg.cholesky(schur)
    trail = apply_inverse(factor, left_side)
    factor_list = [factor]
    left_list = [left_side]
    return (factor, trail, jnp.stack(factor_list), jnp.stack(left_list))


def backward_layers(flow, factors, lefts, grads, coupling, damping):
    layer_dev = grads.shape[0]
    solved = [None] * layer_dev
    penalty = jnp.zeros((grads.shape[1],), jnp.float32)
    for within in reversed(range(layer_dev)):
        vector = apply_inverse(factors[within], lefts[within] - flow)
        flow = jnp.dot(vector, coupling[within].T, precision=lax.Precision.HIGHEST)
        penalty = penalty + damping[within] * jnp.sum(vector * vector, axis=1)
        solved[within] = vector
    return (flow, penalty, jnp.stack(solved))


def on_device(grads, labeled, damping):
    layer_dev, row_count, sketch_width = grads.shape
    groups = lax.axis_size("layer")
    group_index = lax.axis_index("layer")
    cand_total = row_count * lax.axis_size(EX)
    keep_mask = (labeled > 0)[None, :, None]
    masked = jnp.where(keep_mask, grads, jnp.zeros_like(grads))
    before = from_behind(masked[layer_dev - 1], "layer", 1)
    prior_rows = jnp.concatenate([before[None], masked[: layer_dev - 1]], 0)
    diag_terms = jnp.einsum("lnk,lnm->lkm", masked, grads, preferred_element_type=jnp.float32)
    cross_terms = jnp.einsum("lnk,lnm->lkm", prior_rows, grads, preferred_element_type=jnp.float32)
    packed_total, cross_total = packed_total_2(
        (pack_upper(diag_terms), cross_terms), (("ex_0", "ex_1"), "ex_2")
    )
    diag_total = unpack_upper(packed_total, sketch_width)
    identity = jnp.eye(sketch_width, dtype=jnp.float32)
    diagonal = diag_total / cand_total + damping[:, None, None] * identity
    coupling = cross_total / cand_total
    zero_rows = jnp.zeros((row_count, sketch_width), jnp.float32)
    zero_vector = jnp.zeros((row_count,), jnp.float32)
    inbound = (identity, zero_rows)
    state = inbound
    kept = (
        jnp.zeros((layer_dev, sketch_width, sketch_width), jnp.float32),
        jnp.zeros((layer_dev, row_count, sketch_width), jnp.float32),
    )
    for section in range(groups):

        def active_forward():
            return forward_layers(inbound[0], inbound[1], grads, diagonal, coupling)

        def resting_forward():
            return state + kept

        result = lax.cond(group_index == section, active_forward, resting_forward)
        state = result[:2]
        kept = result[2:]
        if section + 1 < groups:
            arrived = from_behind((state[0], state[1]), "layer", 1)
            inbound = tuple(arrived)
    back_in = zero_rows
    back_state = (zero_rows, zero_vector)
    solved = jnp.zeros((layer_dev, row_count, sketch_width), jnp.float32)
    for section in reversed(range(groups)):

        def active_backward():
            flow, penalty, vectors = backward_layers(
                back_in, kept[0], kept[1], grads, coupling, damping
            )
            return (flow, penalty, vectors)

        def resting_backward():
            return back_state + (solved,)

        result = lax.cond(group_index == section, active_backward, resting_backward)
        back_state = result[:2]
        solved = result[2]
        if section > 0:
            back_in = from_behind(back_state[0], "layer", -1)
    own_gain = jnp.sum(grads.astype(jnp.float32) * solved, axis=(0, 2))
    gain, penalty = (total_of_pieces(own_gain, "layer"), total_of_pieces(back_state[1], "layer"))
    score = (gain - penalty) / (1.0 + gain)
    return (solved, score)


def solution(mesh):
    torus = Mesh(
        mesh.devices.reshape(mesh.shape["layer"], 8, 4, 4), ("layer", "ex_0", "ex_1", "ex_2")
    )
    in_specs = (P("layer", EX, None), P(EX), P("layer"))
    out_specs = (P("layer", EX, None), P(EX))
    return jax.shard_map(
        on_device, mesh=torus, in_specs=in_specs, out_specs=out_specs, check_vma=False
    )
```

profile of v0, /device:TPU:8, one launch (start us, length us, event | category | flops | bytes accessed | tf_op | source)
XLA Modules:
  0.0 634.7 jit_solution(13497566494349045410)
XLA Ops:
  11.0 25.0 %all_to_all.28 = f32[4,32,3200]{2,1,0:T(8,128)S(1)} all-to-all(f32[4,32,3200]{2,1,0:T(8,128)S(1)} %copy.28), channel_id=1, replica_groups=mesh['layer'=2,'ex_0'=8,'ex_1'=4,'ex_2'=4] {'ex_2'}, dimensions={0} | all-to-all | bytes 3276800 | tf_op jit(solution)/shard_map/all_to_all | solution.py:48
  36.4 24.3 %all_to_all.29 = f32[32,1,3200]{2,1,0:T(1,128)S(1)} all-to-all(f32[32,1,3200]{2,1,0:T(1,128)S(1)} %all_to_all.19), channel_id=1, replica_groups=mesh['layer'=2,'ex_0'=8,'ex_1'=4,'ex_2'=4] {'ex_0','ex_1'}, dimensions={0} | all-to-all | bytes 819200 | tf_op jit(solution)/shard_map/all_to_all | solution.py:55
  61.2 18.0 %all_to_all.30 = f32[32,1,3200]{2,1,0:T(1,128)S(1)} all-to-all(f32[32,1,3200]{2,1,0:T(1,128)S(1)} %broadcast_in_dim.42), channel_id=1, replica_groups=mesh['layer'=2,'ex_0'=8,'ex_1'=4,'ex_2'=4] {'ex_0','ex_1'}, dimensions={0} | all-to-all | bytes 819200 | tf_op jit(solution)/shard_map/all_to_all | solution.py:25
  80.5 3.6 all-to-all-start.3
  86.4 15.9 %all-to-all-done.3 = f32[4,32,3200]{2,1,0:T(8,128)S(1)} async-done(((f32[4,32,3200]{2,1,0:T(8,128)}), f32[4,32,3200]{2,1,0:T(8,128)S(1)}, u32[]{:S(2)}, u32[]{:S(2)}) %all-to-all-start.3) | async-done | bytes 1638432 | tf_op jit(solution)/shard_map/all_to_all | solution.py:25
  118.2 231.0 %conditional.4 = (f32[512,512]{1,0:T(8,128)}, f32[256,512]{0,1:T(8,128)}, f32[1,512,512]{2,1,0:T(8,128)}, f32[1,256,512]{2,1,0:T(8,128)}) conditional(s32[]{:T(128)} %convert_element_type.46, f32[512,512]{1,0:T(8,128)} %fusion.200, (f32[1,512,512]{1,2,0:T(8,128)S(1)}, f32[1,512,512]{2,1,0:T(8,128)S(1)}, f32[512,512]{1,0:T(8,128)}, ...), branch_computations={%region_2.3_spmd, %region_3.16_spmd} | conditional | flops 4837475328 | bytes 48111140 | solution.py:175
  120.3 10.7 %while.16 = (s32[]{:T(128)}, f32[512,512]{1,0:T(8,128)S(1)}, s32[4,2]{0,1:T(2,128)S(1)}, f32[4,128,128]{2,1,0:T(8,128)}, s32[]{:T(128)}) while((s32[]{:T(128)}, f32[512,512]{1,0:T(8,128)S(1)}, s32[4,2]{0,1:T(2,128)S(1)}, f32[4,128,128]{2,1,0:T(8,128)}, s32[]{:T(128)}) %tuple.165), condition=%wide.while_cond, body=%wide.while_body.sunk | while | flops 2 | bytes 132705 | solution.py:79
  131.1 41.1 %custom-call.37 = f32[4,128,128]{1,2,0:T(8,128)} custom-call(f32[4,128,128]{2,1,0:T(8,128)} %get-tuple-element.142), custom_call_target="InvertDiagBlocksLowerTriangular" | custom-call | tf_op jit(solution)/shard_map/cond/branch_1_fun/jit(_solve_triangular)/triangular_solve | solution.py:79
  182.8 11.7 %cholesky.286 = f32[128,128]{1,0:T(8,128)S(1)} custom-call(f32[128,128]{1,0:T(8,128)S(1)} %cholesky.426), custom_call_target="Cholesky" | custom-call | tf_op jit(solution)/shard_map/cond/branch_1_fun/jit(cholesky)/cholesky | solution.py:122
  194.7 9.8 %custom-call.38 = f32[1,128,128]{1,2,0:T(8,128)S(1)} custom-call(f32[1,128,128]{2,1,0:T(8,128)S(1)} %get-tuple-element.242), custom_call_target="InvertDiagBlocksLowerTriangular" | custom-call | tf_op jit(solution)/shard_map/cond/branch_1_fun/jit(cholesky)/cholesky | solution.py:122
  207.7 11.9 %cholesky.305 = f32[128,128]{1,0:T(8,128)S(1)} custom-call(f32[128,128]{1,0:T(8,128)S(1)} %cholesky.430), custom_call_target="Cholesky" | custom-call | tf_op jit(solution)/shard_map/cond/branch_1_fun/jit(cholesky)/cholesky | solution.py:122
  221.6 9.8 %custom-call.39 = f32[1,128,128]{1,2,0:T(8,128)S(1)} custom-call(f32[1,128,128]{2,1,0:T(8,128)S(1)} %get-tuple-element.239), custom_call_target="InvertDiagBlocksLowerTriangular" | custom-call | tf_op jit(solution)/shard_map/cond/branch_1_fun/jit(cholesky)/cholesky | solution.py:122
  234.5 13.2 %cholesky.326 = f32[128,128]{1,0:T(8,128)} custom-call(f32[128,128]{1,0:T(8,128)} %cholesky.435), custom_call_target="Cholesky" | custom-call | tf_op jit(solution)/shard_map/cond/branch_1_fun/jit(cholesky)/cholesky | solution.py:122
  250.5 11.5 %custom-call.40 = f32[1,128,128]{1,2,0:T(8,128)} custom-call(f32[1,128,128]{2,1,0:T(8,128)} %get-tuple-element.236), custom_call_target="InvertDiagBlocksLowerTriangular" | custom-call | tf_op jit(solution)/shard_map/cond/branch_1_fun/jit(cholesky)/cholesky | solution.py:122
  264.3 11.7 %cholesky.343 = f32[128,128]{1,0:T(8,128)S(1)} custom-call(f32[128,128]{1,0:T(8,128)S(1)} %convolution_subtract_fusion.13), custom_call_target="Cholesky" | custom-call | tf_op jit(solution)/shard_map/cond/branch_1_fun/jit(cholesky)/cholesky | solution.py:122
  279.6 14.1 %while.17 = (s32[]{:T(128)}, f32[512,512]{1,0:T(8,128)}, s32[4,2]{0,1:T(2,128)S(1)}, f32[4,128,128]{2,1,0:T(8,128)}, s32[]{:T(128)}) while((s32[]{:T(128)}, f32[512,512]{1,0:T(8,128)}, s32[4,2]{0,1:T(2,128)S(1)}, f32[4,128,128]{2,1,0:T(8,128)}, s32[]{:T(128)}) %tuple.183), condition=%wide.while_cond.2, body=%wide.while_body.2.sunk | while | flops 2 | bytes 132705 | solution.py:84
  280.3 2.9 bitcast_dynamic-update-slice_fusion.14
  283.8 2.9 bitcast_dynamic-update-slice_fusion.14
  293.8 41.1 %custom-call.42 = f32[4,128,128]{1,2,0:T(8,128)} custom-call(f32[4,128,128]{2,1,0:T(8,128)} %get-tuple-element.144), custom_call_target="InvertDiagBlocksLowerTriangular" | custom-call | tf_op jit(solution)/shard_map/cond/branch_1_fun/jit(_solve_triangular)/triangular_solve | solution.py:84
  355.8 8.1 %conditional.5 = ((f32[1,512,512]{2,1,0:T(8,128)}, f32[1,256,512]{2,1,0:T(8,128)})) conditional(s32[]{:T(128)} %convert_element_type.47, (f32[1,512,512]{2,1,0:T(8,128)}, f32[1,256,512]{2,1,0:T(8,128)}) %tuple.44, (f32[1,512,512]{1,2,0:T(8,128)S(1)}, f32[1,512,512]{2,1,0:T(8,128)S(1)}, f32[512,512]{1,0:T(8,128)S(1)}, ...), branch_computations={%region_12.17_spmd, %region_13.18_spmd} | conditional | flops 3829466112 | bytes 35395404 | solution.py:175
  366.4 204.5 %collective-permute-done.3 = f32[256,512]{0,1:T(8,128)S(1)} collective-permute-done((f32[256,512]{0,1:T(8,128)S(1)}, f32[256,512]{0,1:T(8,128)S(1)}, u32[]{:S(2)}, u32[]{:S(2)}) %collective-permute-start.3) | collective-permute-done | bytes 524320 | tf_op jit(solution)/shard_map/ppermute | solution.py:13
  570.9 57.8 %conditional.7 = (f32[256]{0:T(256)S(1)}, f32[1,256,512]{1,2,0:T(8,128)}, f32[1,256,512]{2,1,0:T(8,128)S(1)}) conditional(s32[]{:T(128)} %convert_element_type.46, (f32[256]{0:T(256)S(1)}, f32[1,256,512]{1,2,0:T(8,128)}) %tuple.47, (f32[1]{0:T(128)}, f32[1,512,512]{2,1,0:T(8,128)}, f32[1,256,512]{2,1,0:T(8,128)}, f32[256,512]{0,1:T(8,128)S(1)}) %tuple.48), branch_computations={%region_17.22_spmd, %region_18.24_spmd} | conditional | flops 1009057792 | bytes 14028025 | solution.py:195
  572.5 8.2 %while.20 = (s32[]{:T(128)}, f32[512,512]{1,0:T(8,128)S(1)}, s32[4,2]{0,1:T(2,128)S(1)}, f32[4,128,128]{2,1,0:T(8,128)S(1)}, s32[]{:T(128)}) while((s32[]{:T(128)}, f32[512,512]{1,0:T(8,128)S(1)}, s32[4,2]{0,1:T(2,128)S(1)}, f32[4,128,128]{2,1,0:T(8,128)S(1)}, s32[]{:T(128)}) %tuple.156), condition=%wide.while_cond.2.clone.1, body=%wide.while_body.2.clone.1.sunk | while | flops 2 | bytes 131181 | solution.py:84
  580.7 39.3 %custom-call.50 = f32[4,128,128]{1,2,0:T(8,128)S(1)} custom-call(f32[4,128,128]{2,1,0:T(8,128)S(1)} %get-tuple-element.149), custom_call_target="InvertDiagBlocksLowerTriangular" | custom-call | tf_op jit(solution)/shard_map/cond/branch_1_fun/jit(_solve_triangular)/triangular_solve | solution.py:84
  (223 shorter events, 123.4 us)
Async XLA Ops:
  2.4 4.6 collective-permute-start
  5.7 1.3 copy-start
  80.5 21.8 %all-to-all-start.3 = ((f32[4,32,3200]{2,1,0:T(8,128)}), f32[4,32,3200]{2,1,0:T(8,128)S(1)}, u32[]{:S(2)}, u32[]{:S(2)}) async-start(f32[4,32,3200]{2,1,0:T(8,128)} %broadcast_in_dim.43), calls=%async_computation.3 | async-start | bytes 3276800 | tf_op jit(solution)/shard_map/all_to_all | solution.py:25
  102.3 1.2 copy-start.1
  112.2 2.3 copy-start.12
  112.2 2.4 copy-start.14
  114.3 0.8 copy-start.13
  115.1 2.7 copy-start.15
  116.4 1.5 copy-start.3
  172.2 3.4 copy-start.10
  181.8 1.0 copy-start.5
  207.0 0.7 copy-start.8
  293.8 44.1 %copy-start.2 = (f32[512,512]{1,0:T(8,128)S(1)}, f32[512,512]{1,0:T(8,128)}, u32[]{:S(2)}) copy-start(f32[512,512]{1,0:T(8,128)} %get-tuple-element.496) | copy-start | bytes 3145732 | tf_op jit(solution)/shard_map/cond
  334.8 1.8 copy-start.6
  349.2 6.5 %collective-permute-start.1 = (f32[512,512]{1,0:T(8,128)}, f32[512,512]{1,0:T(8,128)S(1)}, u32[]{:S(2)}, u32[]{:S(2)}) collective-permute-start(f32[512,512]{1,0:T(8,128)} %get-tuple-element.79), channel_id=1, source_target_pairs={{0,128},{1,129},{2,130},{3,131},{4,132},{5,133},{6,134},{7,135},{8... | collective-permute-start | bytes 3145736 | tf_op jit(solution)/shard_map/ppermute | solution.py:13
  352.6 3.1 collective-permute-start.2
  365.0 205.9 %collective-permute-start.3 = (f32[256,512]{0,1:T(8,128)S(1)}, f32[256,512]{0,1:T(8,128)S(1)}, u32[]{:S(2)}, u32[]{:S(2)}) collective-permute-start(f32[256,512]{0,1:T(8,128)S(1)} %copy.34), channel_id=1, source_target_pairs={{128,0},{129,1},{130,2},{131,3},{132,4},{133,5},{134,6},{135,7},{1... | collective-permute-start | bytes 1572872 | tf_op jit(solution)/shard_map/ppermute | solution.py:13
  628.7 5.6 copy-start.9
where the time goes:
time: 647 us; the launch traced here: 635 us
  waiting for transfers between devices  221 us (34%)
  other arithmetic  220 us (34%)
  blocking collectives  70.9 us (11%)
  local copies, waits for them, and re-layouts  66.9 us (10%)
  matrix products  30.8 us (5%)
  loops' own time  12.1 us (2%)
  starting transfers between devices  10.1 us (2%)
    ppermute x4, waiting for transfers between devices, from_behind(): lax.ppermute(value, axis, [(source, source + steps) for source in range(i...  206 us
    another operation x6, other arithmetic, apply_inverse(): jax.scipy.linalg.solve_triangular(factor, inner, lower=True, trans=1)  83.3 us
    another operation x14, other arithmetic, forward_layers(): factor = jnp.linalg.cholesky(schur)  83.2 us
    another operation x3, other arithmetic, lower_solve(): return jax.scipy.linalg.solve_triangular(factor, right_hand, lower=True)  42.4 us
    all_to_all x1, blocking collectives, sum_at_owner(): lax.all_to_all(parts, axis, split_axis=0, concat_axis=0, tiled=True)  25 us
    all_to_all x1, blocking collectives, summed_rows(): return jnp.sum(lax.all_to_all(own, far, 0, 0, tiled=True), axis=0)  24.3 us
    another operation x25, local copies, waits for them, and re-layouts, apply_inverse(): jax.scipy.linalg.solve_triangular(factor, inner, lower=True, trans=1)  22.2 us
    all_to_all x1, blocking collectives, copy_for_each(): return lax.all_to_all(copies, axis, split_axis=0, concat_axis=0, tiled=True)  18 us
  transfers between devices with their start and end apart: 5, of which 3 were waited for; matrix products, arithmetic and copies ran while one was open for 1% of the time, Pallas kernels for 0%

commit v1 on v0

v1 whole, which is shorter than its diff:
```python
import functools

import jax
import jax.numpy as jnp
from jax import lax
from jax.experimental import pallas as pl
from jax.experimental.pallas import tpu as pltpu
from jax.sharding import Mesh
from jax.sharding import PartitionSpec as P

EX = ("ex_0", "ex_1", "ex_2")
F32, BF16 = jnp.float32, jnp.bfloat16
LANES = 128
RESIDUAL = 0.008
STEPS = 60


def dot(a, b, dims=((1,), (0,)), precision=None):
    return lax.dot_general(a, b, (dims, ((), ())), preferred_element_type=F32, precision=precision)


def split(a):
    high = a.astype(BF16)
    return high, (a - high.astype(F32)).astype(BF16)


def dot_split(a, b, dims=((1,), (0,))):
    total = dot(a[0], b[0], dims)
    if len(b) > 1:
        total = total + dot(a[0], b[1], dims)
    if len(a) > 1:
        total = total + dot(a[1], b[0], dims)
    return total


def gram_kernel(width, core_ref, labeled_ref, own_ref, other_ref, out_ref):
    blocks = width // LANES
    core = core_ref[0]
    keep = (labeled_ref[...] > 0).astype(F32)
    own, other = own_ref[...], other_ref[...]
    own_t = (own.astype(F32).T * keep).astype(BF16)
    first_t = jnp.where(core == 0, own_t, (other.astype(F32).T * keep).astype(BF16))
    last = jnp.where(core == 0, other, own)
    both = jnp.concatenate([own, other], axis=1)
    slab = blocks * LANES + LANES // 2
    for i in range(blocks):
        rows = own_t[i * LANES : (i + 1) * LANES]
        product = dot(rows, both[:, i * LANES : (i + blocks) * LANES])
        for b in range(blocks):
            start = i * slab + b * LANES
            out_ref[start : start + LANES] = product[:, b * LANES : (b + 1) * LANES]
        middle = dot(first_t[i * LANES : (i + 1) * LANES], last[:, i * LANES : (i + 1) * LANES])
        start = i * slab + blocks * LANES
        half = LANES // 2
        out_ref[start : start + half] = jnp.where(core == 0, middle[:half], middle[half:])


def sum_kernel(parts, copies, in_ref, out_ref):
    rows = in_ref.shape[0] // parts
    total = in_ref[:rows]
    for part in range(1, parts):
        total = total + in_ref[part * rows : (part + 1) * rows]
    for copy in range(copies):
        out_ref[copy * rows : (copy + 1) * rows] = total


def eye(width):
    rows = lax.broadcasted_iota(jnp.int32, (width, width), 0)
    return rows == lax.broadcasted_iota(jnp.int32, (width, width), 1)


def invert(s_ref, a_ref, x_ref, r_ref):
    width = s_ref.shape[0]
    unit = eye(width)
    one = unit.astype(F32)
    diagonal = jnp.where(unit, s_ref[...], 0.0)
    scale_row = lax.rsqrt(jnp.sum(diagonal, axis=0, keepdims=True))
    scale_col = lax.rsqrt(jnp.sum(diagonal, axis=1, keepdims=True))
    a_ref[...] = s_ref[...] * scale_col * scale_row

    e = one - a_ref[...]
    e1 = e.astype(BF16)
    e2 = dot(e1, e1).astype(BF16)
    x_ref[...] = one + e
    x_ref[...] += dot(x_ref[...].astype(BF16), e2)
    e4 = dot(e2, e2)
    x_ref[...] += dot(x_ref[...].astype(BF16), e4.astype(BF16))
    contracts = jnp.sum(e4 * e4) < 0.1

    @pl.when(jnp.logical_not(contracts))
    def _():
        largest = jnp.max(jnp.sum(jnp.abs(a_ref[...]), axis=1, keepdims=True))
        x_ref[...] = jnp.where(unit, 1.0 / largest, 0.0)

    r_ref[...] = one - dot_split(split(a_ref[...]), split(x_ref[...]))

    def far(state):
        step, norm = state
        return jnp.logical_and(step < STEPS, norm > RESIDUAL**2)

    def newton(state):
        tile = width // 4

        def advance(t, _):
            at = pl.ds(pl.multiple_of(t * tile, tile), tile)
            x_ref[at, :] += dot(x_ref[at, :], r_ref[...], precision=lax.Precision.HIGHEST)
            return 0

        def residual(t, _):
            at = pl.ds(pl.multiple_of(t * tile, tile), tile)
            r_ref[at, :] = -dot(a_ref[at, :], x_ref[...], precision=lax.Precision.HIGHEST)
            return 0

        lax.fori_loop(0, 4, advance, 0)
        lax.fori_loop(0, 4, residual, 0)
        r_ref[...] += eye(width).astype(F32)
        return state[0] + 1, jnp.sum(r_ref[...] * r_ref[...])

    lax.while_loop(far, newton, (jnp.int32(0), jnp.sum(r_ref[...] * r_ref[...])))
    x_ref[...] += dot(x_ref[...].astype(BF16), r_ref[...].astype(BF16))
    x_ref[...] = x_ref[...] * scale_col * scale_row


def solve_kernel(
    count, core_ref, damp_ref, mine_ref, theirs_ref, own_ref, other_ref,
    solved_ref, score_ref, s_ref, c_ref, ct_ref, d1_ref, a_ref, x_ref, r_ref, y_ref, p0_ref,
):
    core = core_ref[0]
    width = own_ref.shape[1]
    blocks = width // LANES
    half = LANES // 2
    slab = blocks * LANES + half
    near = core == 0
    damp0 = jnp.where(near, damp_ref[0], damp_ref[1])
    damp1 = jnp.where(near, damp_ref[1], damp_ref[0])

    def part(layer, i, start, rows):
        at = i * slab + start
        mine, theirs = mine_ref[at : at + rows], theirs_ref[at : at + rows]
        first, second = (mine, theirs) if layer == 0 else (theirs, mine)
        return jnp.where(near, first, second) * (1.0 / count)

    def put(ref, i, j, block):
        ref[i * LANES : (i + 1) * LANES, j * LANES : (j + 1) * LANES] = block

    unit = eye(LANES)
    for layer, ref, damp in ((0, s_ref, damp0), (1, d1_ref, damp1)):
        for i in range(blocks):
            for b in range(blocks):
                block = part(layer, i, b * LANES, LANES)
                j = i + b
                if b == 0:
                    put(ref, i, i, block + jnp.where(unit, damp, 0.0))
                elif j < blocks:
                    put(ref, i, j, block)
                    put(ref, j, i, block.T)
                elif layer == 0:
                    put(c_ref, i, j - blocks, block)
                    put(ct_ref, j - blocks, i, block.T)
                else:
                    put(ct_ref, i, j - blocks, block)
                    put(c_ref, j - blocks, i, block.T)
    for i in range(blocks):
        block = jnp.concatenate([part(0, i, blocks * LANES, half), part(1, i, blocks * LANES, half)], 0)
        put(c_ref, i, i, block)
        put(ct_ref, i, i, block.T)

    def section(layer, _):
        invert(s_ref, a_ref, x_ref, r_ref)

        @pl.when(layer == 0)
        def _():
            p0_ref[...] = x_ref[...]
            y_ref[...] = dot_split(split(x_ref[...]), split(c_ref[...]))
            s_ref[...] = d1_ref[...] - dot_split(split(ct_ref[...]), split(y_ref[...]))

        return 0

    lax.fori_loop(0, 2, section, 0)
    own, other = own_ref[...], other_ref[...]
    g0 = jnp.where(near, own, other)
    g1 = jnp.where(near, other, own)
    y = split(y_ref[...])
    left = g1.astype(F32) - dot_split((g0,), y)
    z1 = dot_split(split(left), split(x_ref[...]))
    z0 = dot_split((g0,), split(p0_ref[...])) - dot_split(split(z1), y, ((1,), (1,)))
    solved_ref[...] = jnp.where(near, z0, z1)
    gain = g0.astype(F32) * z0 + g1.astype(F32) * z1
    penalty = damp0 * (z0 * z0) + damp1 * (z1 * z1)

    def candidate_sum(terms):
        folded = terms[:, :LANES]
        for b in range(1, blocks):
            folded = folded + terms[:, b * LANES : (b + 1) * LANES]
        return jnp.sum(folded.T, axis=0, keepdims=True)

    gain, penalty = candidate_sum(gain), candidate_sum(penalty)
    score_ref[...] = (gain - penalty) / (1.0 + gain)


SMEM = pl.BlockSpec(memory_space=pltpu.SMEM)
VMEM = pl.BlockSpec(memory_space=pltpu.VMEM)


def exchanged(array, axis):
    devices = lax.axis_size(axis)
    parts = lax.all_to_all(array.reshape(devices, 1, -1), axis, 0, 0, tiled=True)
    return parts.reshape(array.shape)


def on_device(grads, labeled, damping):
    _, row_count, width = grads.shape
    count = row_count * lax.axis_size(EX)
    core = lax.axis_index("layer").astype(jnp.int32).reshape(1)
    swap = [(0, 1), (1, 0)]
    own = grads[0]
    other = lax.ppermute(own, "layer", swap)
    damp = jnp.concatenate([damping, lax.ppermute(damping, "layer", swap)])
    blocks = width // LANES
    slab = blocks * LANES + LANES // 2
    far, near = lax.axis_size(("ex_0", "ex_1")), lax.axis_size("ex_2")

    products = pl.pallas_call(
        functools.partial(gram_kernel, width),
        out_shape=jax.ShapeDtypeStruct((blocks * slab, LANES), F32),
        in_specs=[SMEM, VMEM, VMEM, VMEM],
        out_specs=VMEM,
    )(core, labeled.reshape(1, row_count), own, other)
    arrived = exchanged(products, "ex_2")
    slab_part = pl.pallas_call(
        functools.partial(sum_kernel, near, 1),
        out_shape=jax.ShapeDtypeStruct((slab, LANES), F32),
        in_specs=[VMEM],
        out_specs=VMEM,
    )(arrived)
    arrived = exchanged(slab_part, ("ex_0", "ex_1"))
    piece = pl.pallas_call(
        functools.partial(sum_kernel, far, far),
        out_shape=jax.ShapeDtypeStruct((slab, LANES), F32),
        in_specs=[VMEM],
        out_specs=VMEM,
    )(arrived)
    whole = exchanged(piece, ("ex_0", "ex_1"))
    copies = jnp.broadcast_to(whole[None], (near, slab, LANES)).reshape(near * slab, LANES)
    mine = exchanged(copies, "ex_2")
    theirs = lax.ppermute(mine, "layer", swap)

    square = pltpu.VMEM((width, width), F32)
    solved, score = pl.pallas_call(
        functools.partial(solve_kernel, count),
        out_shape=(
            jax.ShapeDtypeStruct((row_count, width), F32),
            jax.ShapeDtypeStruct((1, row_count), F32),
        ),
        in_specs=[SMEM, SMEM, VMEM, VMEM, VMEM, VMEM],
        out_specs=(VMEM, VMEM),
        scratch_shapes=[square] * 9,
    )(core, damp, mine, theirs, own, other)
    return solved[None], score.reshape(row_count)


def solution(mesh):
    torus = Mesh(
        mesh.devices.reshape(mesh.shape["layer"], 8, 4, 4), ("layer", "ex_0", "ex_1", "ex_2")
    )
    in_specs = (P("layer", EX, None), P(EX), P("layer"))
    out_specs = (P("layer", EX, None), P(EX))
    return jax.shard_map(
        on_device, mesh=torus, in_specs=in_specs, out_specs=out_specs, check_vma=False
    )
```

time: 647 us -> 197 us (0.30)
  the two profiles are of different devices: /device:TPU:8 before, /device:TPU:1 now
where the time goes in v1:
time: 197 us; the launch traced here: 194 us
  Pallas kernels  105 us (53%)
  blocking collectives  72.5 us (37%)
  starting transfers between devices  8.03 us (4%)
  waiting for transfers between devices  3.2 us (2%)
  local copies, waits for them, and re-layouts  2.34 us (1%)
    pallas_call x1, Pallas kernels, on_device(): pl.pallas_call(functools.partial(solve_kernel, count), out_shape=(jax.Sha...  98.6 us
    all_to_all x4, blocking collectives, exchanged(): lax.all_to_all(array.reshape(devices, 1, -1), axis, 0, 0, tiled=True)  72.5 us
    ppermute x1, starting transfers between devices, on_device(): theirs = lax.ppermute(mine, 'layer', swap)  4.74 us
  transfers between devices with their start and end apart: 3, of which 2 were waited for; matrix products, arithmetic and copies ran while one was open for 1% of the time, Pallas kernels for 0%

profile of v1, /device:TPU:1, one launch (start us, length us, event | category | flops | bytes accessed | tf_op | source)
XLA Modules:
  0.0 193.6 jit_solution(15161808724296176228)
XLA Ops:
  0.6 3.3 %collective-permute-start.1 = (bf16[256,512]{1,0:T(8,128)(2,1)}, bf16[256,512]{1,0:T(8,128)(2,1)S(1)}, u32[]{:S(2)}, u32[]{:S(2)}) collective-permute-start(bf16[256,512]{1,0:T(8,128)(2,1)} %bitcast.20), channel_id=1, source_target_pairs={{0,128},{128,0},{1,129},{129,1},{2,130},{130,2},{3,131},{131,3},{4... | collective-permute-start | bytes 786440 | tf_op jit(solution)/shard_map/ppermute | solution.py:217
  3.9 1.4 collective-permute-done.1.other_ref
  5.3 0.0 copy-start.2
  5.3 0.7 copy-done.2
  6.0 2.5 %shard_map.50 = f32[2304,128]{1,0:T(8,128)} custom-call(s32[1]{0:T(128)} %bitcast.core_ref, s32[1,256]{1,0:T(1,128)} %bitcast.23, bf16[256,512]{1,0:T(8,128)(2,1)} %bitcast.21, bf16[256,512]{1,0:T(8,128)(2,1)} %copy-done.2), custom_call_target="tpu_custom_call" | custom-call | tf_op jit(solution)/shard_map/pallas_call | solution.py:223
  8.5 20.6 %all_to_all.20 = f32[4,1,73728]{2,1,0:T(1,128)} all-to-all(f32[4,1,73728]{2,1,0:T(1,128)} %bitcast.15), channel_id=1, replica_groups=mesh['layer'=2,'ex_0'=8,'ex_1'=4,'ex_2'=4] {'ex_2'}, dimensions={0} | all-to-all | bytes 2359296 | tf_op jit(solution)/shard_map/all_to_all | solution.py:207
  29.1 2.0 %shard_map.51 = f32[576,128]{1,0:T(8,128)} custom-call(f32[2304,128]{1,0:T(8,128)} %bitcast.14), custom_call_target="tpu_custom_call" | custom-call | tf_op jit(solution)/shard_map/pallas_call | solution.py:230
  31.1 20.5 %all_to_all.21 = f32[32,1,2304]{2,1,0:T(1,128)} all-to-all(f32[32,1,2304]{2,1,0:T(1,128)} %bitcast.18), channel_id=1, replica_groups=mesh['layer'=2,'ex_0'=8,'ex_1'=4,'ex_2'=4] {'ex_0','ex_1'}, dimensions={0} | all-to-all | bytes 589824 | tf_op jit(solution)/shard_map/all_to_all | solution.py:207
  51.6 1.7 shard_map.52
  53.3 16.3 %all_to_all.22 = f32[32,1,2304]{2,1,0:T(1,128)S(1)} all-to-all(f32[32,1,2304]{2,1,0:T(1,128)} %bitcast.17), channel_id=1, replica_groups=mesh['layer'=2,'ex_0'=8,'ex_1'=4,'ex_2'=4] {'ex_0','ex_1'}, dimensions={0} | all-to-all | bytes 589824 | tf_op jit(solution)/shard_map/all_to_all | solution.py:207
  69.7 0.6 broadcast_in_dim.11
  70.3 15.1 %all_to_all.23 = f32[4,1,73728]{2,1,0:T(1,128)S(1)} all-to-all(f32[4,1,73728]{2,1,0:T(1,128)S(1)} %broadcast_in_dim.11), channel_id=1, replica_groups=mesh['layer'=2,'ex_0'=8,'ex_1'=4,'ex_2'=4] {'ex_2'}, dimensions={0} | all-to-all | bytes 2359296 | tf_op jit(solution)/shard_map/all_to_all | solution.py:207
  85.4 0.0 copy-start
  85.4 4.7 %collective-permute-start.2 = (f32[2304,128]{1,0:T(8,128)S(1)}, f32[2304,128]{1,0:T(8,128)S(1)}, u32[]{:S(2)}, u32[]{:S(2)}) collective-permute-start(f32[2304,128]{1,0:T(8,128)S(1)} %bitcast.12), channel_id=1, source_target_pairs={{0,128},{128,0},{1,129},{129,1},{2,130},{130,2},{3,131},{131,3},{4... | collective-permute-start | bytes 3538952 | tf_op jit(solution)/shard_map/ppermute | solution.py:246
  90.2 0.0 collective-permute-start
  90.8 1.8 collective-permute-done
  92.6 1.3 pad_maximum_fusion.damp_ref
  94.0 0.0 collective-permute-done.2.theirs_ref
  94.0 0.0 copy-done
  94.0 0.0 copy-start.1
  94.0 1.0 copy-done.1
  95.0 98.6 %shard_map.53 = (f32[256,512]{1,0:T(8,128)}, f32[1,256]{1,0:T(1,128)}) custom-call(s32[1]{0:T(128)} %bitcast.core_ref, f32[2]{0:T(128)} %pad_maximum_fusion.damp_ref, f32[2304,128]{1,0:T(8,128)} %bitcast.13, f32[2304,128]{1,0:T(8,128)} %copy-done.1, bf16[256,512]{1,0:T(8,128)(2,1)} %bitcast.22, bf16[256,512]{1,0:T(8,128)(2,1)} %copy-done.2), custom_call_target="tpu_custom_call" | custom-call | tf_op jit(solution)/shard_map/pallas_call | solution.py:249
Async XLA Ops:
  0.6 4.7 %collective-permute-start.1 = (bf16[256,512]{1,0:T(8,128)(2,1)}, bf16[256,512]{1,0:T(8,128)(2,1)S(1)}, u32[]{:S(2)}, u32[]{:S(2)}) collective-permute-start(bf16[256,512]{1,0:T(8,128)(2,1)} %bitcast.20), channel_id=1, source_target_pairs={{0,128},{128,0},{1,129},{129,1},{2,130},{130,2},{3,131},{131,3},{4... | collective-permute-start | bytes 786440 | tf_op jit(solution)/shard_map/ppermute | solution.py:217
  5.3 0.7 copy-start.2
  85.4 8.6 %copy-start = (f32[4,1,73728]{2,1,0:T(1,128)}, f32[4,1,73728]{2,1,0:T(1,128)S(1)}, u32[]{:S(2)}) copy-start(f32[4,1,73728]{2,1,0:T(1,128)S(1)} %all_to_all.23) | copy-start | bytes 3538948
  85.4 8.6 %collective-permute-start.2 = (f32[2304,128]{1,0:T(8,128)S(1)}, f32[2304,128]{1,0:T(8,128)S(1)}, u32[]{:S(2)}, u32[]{:S(2)}) collective-permute-start(f32[2304,128]{1,0:T(8,128)S(1)} %bitcast.12), channel_id=1, source_target_pairs={{0,128},{128,0},{1,129},{129,1},{2,130},{130,2},{3,131},{131,3},{4... | collective-permute-start | bytes 3538952 | tf_op jit(solution)/shard_map/ppermute | solution.py:246
  90.2 2.5 %collective-permute-start = (f32[1]{0:T(128)}, f32[1]{0:T(128)}, u32[]{:S(2)}, u32[]{:S(2)}) collective-permute-start(f32[1]{0:T(128)} %param.5), channel_id=1, source_target_pairs={{0,128},{128,0},{1,129},{129,1},{2,130},{130,2},{3,131},{131,3},{4... | collective-permute-start | bytes 20 | tf_op jit(solution)/shard_map/ppermute | solution.py:218
  94.0 1.0 copy-start.1

commit v2 on v1

--- a/solution.py
+++ b/solution.py
@@ -122,7 +122,7 @@
 
 
 def solve_kernel(
-    count, core_ref, damp_ref, mine_ref, theirs_ref, own_ref, other_ref,
+    count, core_ref, damp_ref, damp_other_ref, mine_ref, theirs_ref, own_ref, other_ref,
     solved_ref, score_ref, s_ref, c_ref, ct_ref, d1_ref, a_ref, x_ref, r_ref, y_ref, p0_ref,
 ):
     core = core_ref[0]
@@ -131,8 +131,8 @@
     half = LANES // 2
     slab = blocks * LANES + half
     near = core == 0
-    damp0 = jnp.where(near, damp_ref[0], damp_ref[1])
-    damp1 = jnp.where(near, damp_ref[1], damp_ref[0])
+    damp0 = jnp.where(near, damp_ref[0], damp_other_ref[0])
+    damp1 = jnp.where(near, damp_other_ref[0], damp_ref[0])
 
     def part(layer, i, start, rows):
         at = i * slab + start
@@ -215,10 +215,12 @@
     swap = [(0, 1), (1, 0)]
     own = grads[0]
     other = lax.ppermute(own, "layer", swap)
-    damp = jnp.concatenate([damping, lax.ppermute(damping, "layer", swap)])
+    damp = lax.ppermute(damping, "layer", swap)
     blocks = width // LANES
     slab = blocks * LANES + LANES // 2
-    far, near = lax.axis_size(("ex_0", "ex_1")), lax.axis_size("ex_2")
+    far, near = lax.axis_size("ex_0"), lax.axis_size(("ex_1", "ex_2"))
+
+    piece_rows = blocks * slab // near
 
     products = pl.pallas_call(
         functools.partial(gram_kernel, width),
@@ -226,23 +228,23 @@
         in_specs=[SMEM, VMEM, VMEM, VMEM],
         out_specs=VMEM,
     )(core, labeled.reshape(1, row_count), own, other)
-    arrived = exchanged(products, "ex_2")
+    arrived = exchanged(products, ("ex_1", "ex_2"))
     slab_part = pl.pallas_call(
         functools.partial(sum_kernel, near, 1),
-        out_shape=jax.ShapeDtypeStruct((slab, LANES), F32),
+        out_shape=jax.ShapeDtypeStruct((piece_rows, LANES), F32),
         in_specs=[VMEM],
         out_specs=VMEM,
     )(arrived)
-    arrived = exchanged(slab_part, ("ex_0", "ex_1"))
+    arrived = exchanged(slab_part, "ex_0")
     piece = pl.pallas_call(
         functools.partial(sum_kernel, far, far),
-        out_shape=jax.ShapeDtypeStruct((slab, LANES), F32),
+        out_shape=jax.ShapeDtypeStruct((piece_rows, LANES), F32),
         in_specs=[VMEM],
         out_specs=VMEM,
     )(arrived)
-    whole = exchanged(piece, ("ex_0", "ex_1"))
-    copies = jnp.broadcast_to(whole[None], (near, slab, LANES)).reshape(near * slab, LANES)
-    mine = exchanged(copies, "ex_2")
+    whole = exchanged(piece, "ex_0")
+    copies = jnp.broadcast_to(whole[None], (near, piece_rows, LANES)).reshape(blocks * slab, LANES)
+    mine = exchanged(copies, ("ex_1", "ex_2"))
     theirs = lax.ppermute(mine, "layer", swap)
 
     square = pltpu.VMEM((width, width), F32)
@@ -252,10 +254,10 @@
             jax.ShapeDtypeStruct((row_count, width), F32),
             jax.ShapeDtypeStruct((1, row_count), F32),
         ),
-        in_specs=[SMEM, SMEM, VMEM, VMEM, VMEM, VMEM],
+        in_specs=[SMEM, SMEM, SMEM, VMEM, VMEM, VMEM, VMEM],
         out_specs=(VMEM, VMEM),
         scratch_shapes=[square] * 9,
-    )(core, damp, mine, theirs, own, other)
+    )(core, damping, damp, mine, theirs, own, other)
     return solved[None], score.reshape(row_count)
 
 

time: 197 us -> 188 us (0.954)
  the two profiles are of different devices: /device:TPU:1 before, /device:TPU:8 now
where the time goes in v2:
time: 188 us; the launch traced here: 185 us
  Pallas kernels  105 us (56%)
  blocking collectives  72.1 us (38%)
  waiting for transfers between devices  3.41 us (2%)
  local copies, waits for them, and re-layouts  2.33 us (1%)
    pallas_call x1, Pallas kernels, on_device(): pl.pallas_call(functools.partial(solve_kernel, count), out_shape=(jax.Sha...  99.3 us
    all_to_all x4, blocking collectives, exchanged(): lax.all_to_all(array.reshape(devices, 1, -1), axis, 0, 0, tiled=True)  72.1 us
  transfers between devices with their start and end apart: 3, of which 2 were waited for; matrix products, arithmetic and copies ran while one was open for 0% of the time, Pallas kernels for 0%

profile of v2, /device:TPU:8, one launch (start us, length us, event | category | flops | bytes accessed | tf_op | source)
XLA Modules:
  0.0 185.0 jit_solution(2996803700723108626)
XLA Ops:
  0.6 0.1 collective-permute-start.1
  0.7 1.7 collective-permute-done.1.other_ref
  2.5 0.0 copy-start.2
  2.5 0.7 copy-done.2
  3.2 2.5 %shard_map.50 = f32[2304,128]{1,0:T(8,128)} custom-call(s32[1]{0:T(128)} %bitcast.core_ref, s32[1,256]{1,0:T(1,128)} %bitcast.23, bf16[256,512]{1,0:T(8,128)(2,1)} %bitcast.17, bf16[256,512]{1,0:T(8,128)(2,1)} %copy-done.2), custom_call_target="tpu_custom_call" | custom-call | tf_op jit(solution)/shard_map/pallas_call | solution.py:225
  5.7 24.7 %all_to_all.20 = f32[16,1,18432]{2,1,0:T(1,128)} all-to-all(f32[16,1,18432]{2,1,0:T(1,128)} %bitcast.15), channel_id=1, replica_groups=mesh['layer'=2,'ex_0'=8,'ex_1'=4,'ex_2'=4] {'ex_1','ex_2'}, dimensions={0} | all-to-all | bytes 2359296 | tf_op jit(solution)/shard_map/all_to_all | solution.py:207
  30.3 2.0 %shard_map.51 = f32[144,128]{1,0:T(8,128)} custom-call(f32[2304,128]{1,0:T(8,128)} %bitcast.14), custom_call_target="tpu_custom_call" | custom-call | tf_op jit(solution)/shard_map/pallas_call | solution.py:232
  32.3 17.0 %all_to_all.21 = f32[8,1,2304]{2,1,0:T(1,128)} all-to-all(f32[8,1,2304]{2,1,0:T(1,128)} %bitcast.19), channel_id=1, replica_groups=mesh['layer'=2,'ex_0'=8,'ex_1'=4,'ex_2'=4] {'ex_0'}, dimensions={0} | all-to-all | bytes 147456 | tf_op jit(solution)/shard_map/all_to_all | solution.py:207
  49.3 1.5 shard_map.52
  50.9 11.7 %all_to_all.22 = f32[8,1,2304]{2,1,0:T(1,128)S(1)} all-to-all(f32[8,1,2304]{2,1,0:T(1,128)} %bitcast.22), channel_id=1, replica_groups=mesh['layer'=2,'ex_0'=8,'ex_1'=4,'ex_2'=4] {'ex_0'}, dimensions={0} | all-to-all | bytes 147456 | tf_op jit(solution)/shard_map/all_to_all | solution.py:207
  62.6 0.6 broadcast_in_dim.11
  63.2 18.7 %all_to_all.23 = f32[16,1,18432]{2,1,0:T(1,128)S(1)} all-to-all(f32[16,1,18432]{2,1,0:T(1,128)S(1)} %broadcast_in_dim.11), channel_id=1, replica_groups=mesh['layer'=2,'ex_0'=8,'ex_1'=4,'ex_2'=4] {'ex_1','ex_2'}, dimensions={0} | all-to-all | bytes 2359296 | tf_op jit(solution)/shard_map/all_to_all | solution.py:207
  81.9 0.0 copy-start
  81.9 0.0 collective-permute-start.2
  81.9 0.5 collective-permute-start
  83.0 1.7 collective-permute-done.damp_other_ref
  84.7 0.0 collective-permute-done.2.theirs_ref
  84.7 0.0 copy-done
  84.7 0.0 copy-start.1
  84.7 1.0 copy-done.1
  85.7 99.3 %shard_map.53 = (f32[256,512]{1,0:T(8,128)}, f32[1,256]{1,0:T(1,128)}) custom-call(s32[1]{0:T(128)} %bitcast.core_ref, f32[1]{0:T(128)S(6)} %copy.8.damp_ref, f32[1]{0:T(128)} %collective-permute-done.damp_other_ref, f32[2304,128]{1,0:T(8,128)} %bitcast.13, f32[2304,128]{1,0:T(8,128)} %copy-done.1, bf16[256,512]{1,0:T(8,128)(2,1)} %bitcast.18, ...), custom_call_target="tpu_custom_call" | custom-call | tf_op jit(solution)/shard_map/pallas_call | solution.py:251
Async XLA Ops:
  0.6 1.8 collective-permute-start.1
  2.5 0.7 copy-start.2
  81.9 2.9 %copy-start = (f32[16,1,18432]{2,1,0:T(1,128)}, f32[16,1,18432]{2,1,0:T(1,128)S(1)}, u32[]{:S(2)}) copy-start(f32[16,1,18432]{2,1,0:T(1,128)S(1)} %all_to_all.23) | copy-start | bytes 3538948
  81.9 2.9 %collective-permute-start.2 = (f32[2304,128]{1,0:T(8,128)S(1)}, f32[2304,128]{1,0:T(8,128)S(1)}, u32[]{:S(2)}, u32[]{:S(2)}) collective-permute-start(f32[2304,128]{1,0:T(8,128)S(1)} %bitcast.12), channel_id=1, source_target_pairs={{0,128},{128,0},{1,129},{129,1},{2,130},{130,2},{3,131},{131,3},{4... | collective-permute-start | bytes 3538952 | tf_op jit(solution)/shard_map/ppermute | solution.py:248
  81.9 2.8 %collective-permute-start = (f32[1]{0:T(128)}, f32[1]{0:T(128)}, u32[]{:S(2)}, u32[]{:S(2)}) collective-permute-start(f32[1]{0:T(128)} %param.5), channel_id=1, source_target_pairs={{0,128},{128,0},{1,129},{129,1},{2,130},{130,2},{3,131},{131,3},{4... | collective-permute-start | bytes 20 | tf_op jit(solution)/shard_map/ppermute | solution.py:218
  84.7 1.0 copy-start.1

commit v3 on v2

--- a/solution.py
+++ b/solution.py
@@ -202,6 +202,10 @@
 VMEM = pl.BlockSpec(memory_space=pltpu.VMEM)
 
 
+def limit(mebibytes):
+    return pltpu.CompilerParams(vmem_limit_bytes=mebibytes * 2**20)
+
+
 def exchanged(array, axis):
     devices = lax.axis_size(axis)
     parts = lax.all_to_all(array.reshape(devices, 1, -1), axis, 0, 0, tiled=True)
@@ -227,6 +231,7 @@
         out_shape=jax.ShapeDtypeStruct((blocks * slab, LANES), F32),
         in_specs=[SMEM, VMEM, VMEM, VMEM],
         out_specs=VMEM,
+        compiler_params=limit(16),
     )(core, labeled.reshape(1, row_count), own, other)
     arrived = exchanged(products, ("ex_1", "ex_2"))
     slab_part = pl.pallas_call(
@@ -234,6 +239,7 @@
         out_shape=jax.ShapeDtypeStruct((piece_rows, LANES), F32),
         in_specs=[VMEM],
         out_specs=VMEM,
+        compiler_params=limit(8),
     )(arrived)
     arrived = exchanged(slab_part, "ex_0")
     piece = pl.pallas_call(
@@ -241,6 +247,7 @@
         out_shape=jax.ShapeDtypeStruct((piece_rows, LANES), F32),
         in_specs=[VMEM],
         out_specs=VMEM,
+        compiler_params=limit(8),
     )(arrived)
     whole = exchanged(piece, "ex_0")
     copies = jnp.broadcast_to(whole[None], (near, piece_rows, LANES)).reshape(blocks * slab, LANES)
@@ -257,6 +264,7 @@
         in_specs=[SMEM, SMEM, SMEM, VMEM, VMEM, VMEM, VMEM],
         out_specs=(VMEM, VMEM),
         scratch_shapes=[square] * 9,
+        compiler_params=limit(32),
     )(core, damping, damp, mine, theirs, own, other)
     return solved[None], score.reshape(row_count)
 

time: 188 us -> 182 us (0.968)
  the two profiles are of different devices: /device:TPU:8 before, /device:TPU:1 now
where the time goes in v3:
time: 182 us; the launch traced here: 179 us
  Pallas kernels  98 us (54%)
  blocking collectives  65.8 us (36%)
  starting transfers between devices  8.26 us (5%)
  waiting for transfers between devices  3.33 us (2%)
  local copies, waits for them, and re-layouts  2.24 us (1%)
    pallas_call x1, Pallas kernels, on_device(): pl.pallas_call(functools.partial(solve_kernel, count), out_shape=(jax.Sha...  97.5 us
    all_to_all x4, blocking collectives, exchanged(): lax.all_to_all(array.reshape(devices, 1, -1), axis, 0, 0, tiled=True)  65.8 us
    ppermute x1, starting transfers between devices, on_device(): theirs = lax.ppermute(mine, 'layer', swap)  4.97 us
  transfers between devices with their start and end apart: 3, of which 2 were waited for; matrix products, arithmetic and copies ran while one was open for 0% of the time, Pallas kernels for 0%

profile of v3, /device:TPU:1, one launch (start us, length us, event | category | flops | bytes accessed | tf_op | source)
XLA Modules:
  0.0 178.9 jit_solution(15805101112695365893)
XLA Ops:
  0.6 3.3 %collective-permute-start.1 = (bf16[256,512]{1,0:T(8,128)(2,1)}, bf16[256,512]{1,0:T(8,128)(2,1)S(1)}, u32[]{:S(2)}, u32[]{:S(2)}) collective-permute-start(bf16[256,512]{1,0:T(8,128)(2,1)} %bitcast.16), channel_id=1, source_target_pairs={{0,128},{128,0},{1,129},{129,1},{2,130},{130,2},{3,131},{131,3},{4... | collective-permute-start | bytes 786440 | tf_op jit(solution)/shard_map/ppermute | solution.py:221
  3.9 1.4 collective-permute-done.1.other_ref
  5.3 0.0 copy-start
  5.3 0.9 copy-done
  6.2 0.0 copy-start.2
  6.2 0.7 copy-done.2
  6.9 0.4 shard_map.50
  7.4 22.9 %all_to_all.20 = f32[16,1,18432]{2,1,0:T(1,128)S(1)} all-to-all(f32[16,1,18432]{2,1,0:T(1,128)S(1)} %bitcast.15), channel_id=1, replica_groups=mesh['layer'=2,'ex_0'=8,'ex_1'=4,'ex_2'=4] {'ex_1','ex_2'}, dimensions={0} | all-to-all | bytes 2359296 | tf_op jit(solution)/shard_map/all_to_all | solution.py:211
  30.3 0.1 shard_map.51
  30.3 15.4 %all_to_all.21 = f32[8,1,2304]{2,1,0:T(1,128)S(1)} all-to-all(f32[8,1,2304]{2,1,0:T(1,128)S(1)} %bitcast.19), channel_id=1, replica_groups=mesh['layer'=2,'ex_0'=8,'ex_1'=4,'ex_2'=4] {'ex_0'}, dimensions={0} | all-to-all | bytes 147456 | tf_op jit(solution)/shard_map/all_to_all | solution.py:211
  45.7 9.8 %all_to_all.22 = f32[8,1,2304]{2,1,0:T(1,128)S(1)} all-to-all(f32[8,1,2304]{2,1,0:T(1,128)S(1)} %bitcast.21), channel_id=1, replica_groups=mesh['layer'=2,'ex_0'=8,'ex_1'=4,'ex_2'=4] {'ex_0'}, dimensions={0} | all-to-all | bytes 147456 | tf_op jit(solution)/shard_map/all_to_all | solution.py:211
  55.5 0.6 broadcast_in_dim.11
  56.1 0.0 copy-start.1
  56.1 17.7 %all_to_all.23 = f32[16,1,18432]{2,1,0:T(1,128)S(1)} all-to-all(f32[16,1,18432]{2,1,0:T(1,128)S(1)} %broadcast_in_dim.11), channel_id=1, replica_groups=mesh['layer'=2,'ex_0'=8,'ex_1'=4,'ex_2'=4] {'ex_1','ex_2'}, dimensions={0} | all-to-all | bytes 2359296 | tf_op jit(solution)/shard_map/all_to_all | solution.py:211
  73.8 5.0 %collective-permute-start.2 = (f32[2304,128]{1,0:T(8,128)S(1)}, f32[2304,128]{1,0:T(8,128)S(1)}, u32[]{:S(2)}, u32[]{:S(2)}) collective-permute-start(f32[2304,128]{1,0:T(8,128)S(1)} %bitcast.12), channel_id=1, source_target_pairs={{0,128},{128,0},{1,129},{129,1},{2,130},{130,2},{3,131},{131,3},{4... | collective-permute-start | bytes 3538952 | tf_op jit(solution)/shard_map/ppermute | solution.py:255
  78.8 0.0 collective-permute-start
  79.4 2.0 %collective-permute-done.damp_other_ref = f32[1]{0:T(128)} collective-permute-done((f32[1]{0:T(128)}, f32[1]{0:T(128)}, u32[]{:S(2)}, u32[]{:S(2)}) %collective-permute-start) | collective-permute-done | bytes 36 | tf_op jit(solution)/shard_map/ppermute | solution.py:222
  81.4 0.0 collective-permute-done.2.theirs_ref
  81.4 0.0 copy-done.1
  81.4 97.5 %shard_map.53 = (f32[256,512]{1,0:T(8,128)}, f32[1,256]{1,0:T(1,128)}) custom-call(s32[1]{0:T(128)} %bitcast.core_ref, f32[1]{0:T(128)S(6)} %copy.8.damp_ref, f32[1]{0:T(128)} %collective-permute-done.damp_other_ref, f32[2304,128]{1,0:T(8,128)S(1)} %bitcast.13, f32[2304,128]{1,0:T(8,128)S(1)} %collective-permute-done.2.theirs_ref, ...), custom_call_target="tpu_custom_call" | custom-call | tf_op jit(solution)/shard_map/pallas_call | solution.py:258
  (1 shorter events, 0.0 us)
Async XLA Ops:
  0.6 4.7 %collective-permute-start.1 = (bf16[256,512]{1,0:T(8,128)(2,1)}, bf16[256,512]{1,0:T(8,128)(2,1)S(1)}, u32[]{:S(2)}, u32[]{:S(2)}) collective-permute-start(bf16[256,512]{1,0:T(8,128)(2,1)} %bitcast.16), channel_id=1, source_target_pairs={{0,128},{128,0},{1,129},{129,1},{2,130},{130,2},{3,131},{131,3},{4... | collective-permute-start | bytes 786440 | tf_op jit(solution)/shard_map/ppermute | solution.py:221
  5.3 0.9 copy-start
  6.2 0.7 copy-start.2
  56.1 25.3 %copy-start.1 = (bf16[1,256,512]{2,1,0:T(8,128)(2,1)S(1)}, bf16[1,256,512]{2,1,0:T(8,128)(2,1)}, u32[]{:S(2)}) copy-start(bf16[1,256,512]{2,1,0:T(8,128)(2,1)} %param.3) | copy-start | bytes 786436
  73.8 7.6 %collective-permute-start.2 = (f32[2304,128]{1,0:T(8,128)S(1)}, f32[2304,128]{1,0:T(8,128)S(1)}, u32[]{:S(2)}, u32[]{:S(2)}) collective-permute-start(f32[2304,128]{1,0:T(8,128)S(1)} %bitcast.12), channel_id=1, source_target_pairs={{0,128},{128,0},{1,129},{129,1},{2,130},{130,2},{3,131},{131,3},{4... | collective-permute-start | bytes 3538952 | tf_op jit(solution)/shard_map/ppermute | solution.py:255
  78.8 2.6 %collective-permute-start = (f32[1]{0:T(128)}, f32[1]{0:T(128)}, u32[]{:S(2)}, u32[]{:S(2)}) collective-permute-start(f32[1]{0:T(128)} %param.5), channel_id=1, source_target_pairs={{0,128},{128,0},{1,129},{129,1},{2,130},{130,2},{3,131},{131,3},{4... | collective-permute-start | bytes 20 | tf_op jit(solution)/shard_map/ppermute | solution.py:222

commit v4 on v3

--- a/solution.py
+++ b/solution.py
@@ -8,7 +8,8 @@
 from jax.sharding import Mesh
 from jax.sharding import PartitionSpec as P
 
-EX = ("ex_0", "ex_1", "ex_2")
+EX = ("z_hi", "z_lo", "y", "x")
+FAR, NEAR = EX[0], EX[1:]
 F32, BF16 = jnp.float32, jnp.bfloat16
 LANES = 128
 RESIDUAL = 0.008
@@ -212,6 +213,17 @@
     return parts.reshape(array.shape)
 
 
+def summed(array, parts, copies):
+    rows = array.shape[0] // parts
+    return pl.pallas_call(
+        functools.partial(sum_kernel, parts, copies),
+        out_shape=jax.ShapeDtypeStruct((copies * rows, LANES), F32),
+        in_specs=[VMEM],
+        out_specs=VMEM,
+        compiler_params=limit(8),
+    )(array)
+
+
 def on_device(grads, labeled, damping):
     _, row_count, width = grads.shape
     count = row_count * lax.axis_size(EX)
@@ -222,10 +234,7 @@
     damp = lax.ppermute(damping, "layer", swap)
     blocks = width // LANES
     slab = blocks * LANES + LANES // 2
-    far, near = lax.axis_size("ex_0"), lax.axis_size(("ex_1", "ex_2"))
-
-    piece_rows = blocks * slab // near
-
+    pieces, planes = lax.axis_size(NEAR), lax.axis_size(FAR)
     products = pl.pallas_call(
         functools.partial(gram_kernel, width),
         out_shape=jax.ShapeDtypeStruct((blocks * slab, LANES), F32),
@@ -233,25 +242,9 @@
         out_specs=VMEM,
         compiler_params=limit(16),
     )(core, labeled.reshape(1, row_count), own, other)
-    arrived = exchanged(products, ("ex_1", "ex_2"))
-    slab_part = pl.pallas_call(
-        functools.partial(sum_kernel, near, 1),
-        out_shape=jax.ShapeDtypeStruct((piece_rows, LANES), F32),
-        in_specs=[VMEM],
-        out_specs=VMEM,
-        compiler_params=limit(8),
-    )(arrived)
-    arrived = exchanged(slab_part, "ex_0")
-    piece = pl.pallas_call(
-        functools.partial(sum_kernel, far, far),
-        out_shape=jax.ShapeDtypeStruct((piece_rows, LANES), F32),
-        in_specs=[VMEM],
-        out_specs=VMEM,
-        compiler_params=limit(8),
-    )(arrived)
-    whole = exchanged(piece, "ex_0")
-    copies = jnp.broadcast_to(whole[None], (near, piece_rows, LANES)).reshape(blocks * slab, LANES)
-    mine = exchanged(copies, ("ex_1", "ex_2"))
+    partial = summed(exchanged(products, NEAR), pieces, planes)
+    total = summed(exchanged(partial, FAR), planes, pieces)
+    mine = exchanged(total, NEAR)
     theirs = lax.ppermute(mine, "layer", swap)
 
     square = pltpu.VMEM((width, width), F32)
@@ -271,7 +264,7 @@
 
 def solution(mesh):
     torus = Mesh(
-        mesh.devices.reshape(mesh.shape["layer"], 8, 4, 4), ("layer", "ex_0", "ex_1", "ex_2")
+        mesh.devices.reshape(mesh.shape["layer"], 4, 2, 4, 4), ("layer", *EX)
     )
     in_specs = (P("layer", EX, None), P(EX), P("layer"))
     out_specs = (P("layer", EX, None), P(EX))

time: 182 us -> 177 us (0.973)
  the two profiles are of different devices: /device:TPU:1 before, /device:TPU:8 now
where the time goes in v4:
time: 177 us; the launch traced here: 175 us
  Pallas kernels  104 us (59%)
  blocking collectives  63.8 us (36%)
  waiting for transfers between devices  3.55 us (2%)
    pallas_call x1, Pallas kernels, on_device(): pl.pallas_call(functools.partial(solve_kernel, count), out_shape=(jax.Sha...  103 us
    all_to_all x3, blocking collectives, exchanged(): lax.all_to_all(array.reshape(devices, 1, -1), axis, 0, 0, tiled=True)  63.8 us
  transfers between devices with their start and end apart: 3, of which 2 were waited for; matrix products, arithmetic and copies ran while one was open for 0% of the time, Pallas kernels for 0%

profile of v4, /device:TPU:8, one launch (start us, length us, event | category | flops | bytes accessed | tf_op | source)
XLA Modules:
  0.0 174.6 jit_solution(14143612176157510507)
XLA Ops:
  0.6 0.1 collective-permute-start.1
  0.7 1.7 collective-permute-done.1.other_ref
  2.5 0.0 copy-start
  2.5 0.9 copy-done
  3.4 0.0 copy-start.2
  3.4 0.7 copy-done.2
  4.1 0.4 shard_map.50
  4.5 26.8 %all_to_all.15 = f32[32,1,9216]{2,1,0:T(1,128)S(1)} all-to-all(f32[32,1,9216]{2,1,0:T(1,128)S(1)} %bitcast.15), channel_id=1, replica_groups=mesh['layer'=2,'z_hi'=4,'z_lo'=2,'y'=4,'x'=4] {'z_lo','y','x'}, dimensions={0} | all-to-all | bytes 2359296 | tf_op jit(solution)/shard_map/all_to_all | solution.py:212
  31.4 0.1 shard_map.51
  31.4 16.2 %all_to_all.16 = f32[4,1,9216]{2,1,0:T(1,128)S(1)} all-to-all(f32[4,1,9216]{2,1,0:T(1,128)S(1)} %bitcast.19), channel_id=1, replica_groups=mesh['layer'=2,'z_hi'=4,'z_lo'=2,'y'=4,'x'=4] {'z_hi'}, dimensions={0} | all-to-all | bytes 294912 | tf_op jit(solution)/shard_map/all_to_all | solution.py:212
  47.7 0.1 shard_map.52
  47.8 0.0 copy-start.1
  47.8 20.8 %all_to_all.17 = f32[32,1,9216]{2,1,0:T(1,128)S(1)} all-to-all(f32[32,1,9216]{2,1,0:T(1,128)S(1)} %bitcast.14), channel_id=1, replica_groups=mesh['layer'=2,'z_hi'=4,'z_lo'=2,'y'=4,'x'=4] {'z_lo','y','x'}, dimensions={0} | all-to-all | bytes 2359296 | tf_op jit(solution)/shard_map/all_to_all | solution.py:212
  68.5 0.0 collective-permute-start.2
  68.5 0.5 collective-permute-start
  69.7 1.8 %collective-permute-done.damp_other_ref = f32[1]{0:T(128)} collective-permute-done((f32[1]{0:T(128)}, f32[1]{0:T(128)}, u32[]{:S(2)}, u32[]{:S(2)}) %collective-permute-start) | collective-permute-done | bytes 36 | tf_op jit(solution)/shard_map/ppermute | solution.py:234
  71.5 0.0 collective-permute-done.2.theirs_ref
  71.5 0.0 copy-done.1
  71.5 103.1 %shard_map.53 = (f32[256,512]{1,0:T(8,128)}, f32[1,256]{1,0:T(1,128)}) custom-call(s32[1]{0:T(128)} %bitcast.core_ref, f32[1]{0:T(128)S(6)} %copy.8.damp_ref, f32[1]{0:T(128)} %collective-permute-done.damp_other_ref, f32[2304,128]{1,0:T(8,128)S(1)} %bitcast.12, f32[2304,128]{1,0:T(8,128)S(1)} %collective-permute-done.2.theirs_ref, ...), custom_call_target="tpu_custom_call" | custom-call | tf_op jit(solution)/shard_map/pallas_call | solution.py:251
Async XLA Ops:
  0.6 1.8 %collective-permute-start.1 = (bf16[256,512]{1,0:T(8,128)(2,1)}, bf16[256,512]{1,0:T(8,128)(2,1)S(1)}, u32[]{:S(2)}, u32[]{:S(2)}) collective-permute-start(bf16[256,512]{1,0:T(8,128)(2,1)} %bitcast.16), channel_id=1, source_target_pairs={{0,128},{128,0},{1,129},{129,1},{2,130},{130,2},{3,131},{131,3},{4... | collective-permute-start | bytes 786440 | tf_op jit(solution)/shard_map/ppermute | solution.py:233
  2.5 1.0 copy-start
  3.4 0.7 copy-start.2
  47.8 23.8 %copy-start.1 = (bf16[1,256,512]{2,1,0:T(8,128)(2,1)S(1)}, bf16[1,256,512]{2,1,0:T(8,128)(2,1)}, u32[]{:S(2)}) copy-start(bf16[1,256,512]{2,1,0:T(8,128)(2,1)} %param.3) | copy-start | bytes 786436
  68.5 3.0 %collective-permute-start.2 = (f32[2304,128]{1,0:T(8,128)S(1)}, f32[2304,128]{1,0:T(8,128)S(1)}, u32[]{:S(2)}, u32[]{:S(2)}) collective-permute-start(f32[2304,128]{1,0:T(8,128)S(1)} %bitcast.11), channel_id=1, source_target_pairs={{0,128},{128,0},{1,129},{129,1},{2,130},{130,2},{3,131},{131,3},{4... | collective-permute-start | bytes 3538952 | tf_op jit(solution)/shard_map/ppermute | solution.py:248
  68.5 3.0 %collective-permute-start = (f32[1]{0:T(128)}, f32[1]{0:T(128)}, u32[]{:S(2)}, u32[]{:S(2)}) collective-permute-start(f32[1]{0:T(128)} %param.5), channel_id=1, source_target_pairs={{0,128},{128,0},{1,129},{129,1},{2,130},{130,2},{3,131},{131,3},{4... | collective-permute-start | bytes 20 | tf_op jit(solution)/shard_map/ppermute | solution.py:234

commit v5 on v4

v5 whole, which is shorter than its diff:
```python
import functools

import jax
import jax.numpy as jnp
from jax import lax
from jax.experimental import pallas as pl
from jax.experimental.pallas import tpu as pltpu
from jax.sharding import Mesh
from jax.sharding import PartitionSpec as P

EX = ("z_hi", "z_lo", "y", "x")
FAR, NEAR = EX[0], EX[1:]
F32, BF16 = jnp.float32, jnp.bfloat16
LANES = 128
HALF = LANES // 2
RESIDUAL = 0.002
STEPS = 60
TILES = 4
REFINEMENTS = 3


def dot(a, b, dims=((1,), (0,)), precision=None):
    return lax.dot_general(a, b, (dims, ((), ())), preferred_element_type=F32, precision=precision)


def split(a):
    high = a.astype(BF16)
    return high, (a - high.astype(F32)).astype(BF16)


def dot_split(a, b, dims=((1,), (0,))):
    total = dot(a[0], b[0], dims)
    if len(b) > 1:
        total = total + dot(a[0], b[1], dims)
    if len(a) > 1:
        total = total + dot(a[1], b[0], dims)
    return total


def dot_full(out_ref, a_ref, b, base_ref=None, dims=((1,), (0,))):
    tile = a_ref.shape[0] // TILES

    def step(t, _):
        at = pl.ds(pl.multiple_of(t * tile, tile), tile)
        product = dot(a_ref[at, :].astype(F32), b[...], dims, lax.Precision.HIGHEST)
        out_ref[at, :] = product if base_ref is None else base_ref[at, :].astype(F32) - product
        return 0

    lax.fori_loop(0, TILES, step, 0)


def mask_kernel(labeled_ref, own_ref, out_ref):
    keep = (labeled_ref[...] > 0).astype(F32)
    out_ref[...] = (own_ref[...].astype(F32).T * keep).astype(BF16)


def gram_kernel(core_ref, labeled_ref, own_t_ref, own_ref, other_ref, out_ref):
    core = core_ref[0]
    keep = (labeled_ref[...] > 0).astype(F32)
    own_t, own, other = own_t_ref[...], own_ref[...], other_ref[...]
    blocks = own.shape[1] // LANES
    first_t = jnp.where(core == 0, own_t, (other.astype(F32).T * keep).astype(BF16))
    last = jnp.where(core == 0, other, own)
    both = jnp.concatenate([own, other], axis=1)
    slab = blocks * LANES + HALF
    for i in range(blocks):
        rows = own_t[i * LANES : (i + 1) * LANES]
        product = dot(rows, both[:, i * LANES : (i + blocks) * LANES])
        for b in range(blocks):
            start = i * slab + b * LANES
            out_ref[start : start + LANES] = product[:, b * LANES : (b + 1) * LANES]
        middle = dot(first_t[i * LANES : (i + 1) * LANES], last[:, i * LANES : (i + 1) * LANES])
        start = i * slab + blocks * LANES
        out_ref[start : start + HALF] = jnp.where(core == 0, middle[:HALF], middle[HALF:])


def sum_kernel(in_ref, out_ref):
    rows = out_ref.shape[0]
    total = in_ref[:rows]
    for part in range(1, in_ref.shape[0] // rows):
        total = total + in_ref[part * rows : (part + 1) * rows]
    out_ref[...] = total


def total_kernel(*refs):
    out_ref = refs[-1]
    total = refs[0][...]
    for ref in refs[1:-1]:
        total = total + ref[...]
    rows = total.shape[0]
    for copy in range(out_ref.shape[0] // rows):
        out_ref[copy * rows : (copy + 1) * rows] = total


def eye(width):
    rows = lax.broadcasted_iota(jnp.int32, (width, width), 0)
    return rows == lax.broadcasted_iota(jnp.int32, (width, width), 1)


def invert(s_ref, a_ref, x_ref, r_ref, t_ref, refresh=None, known_hard=None):
    width = s_ref.shape[0]

    def scales():
        diagonal = jnp.where(eye(width), s_ref[...], 0.0)
        row = lax.rsqrt(jnp.sum(diagonal, axis=0, keepdims=True))
        return lax.rsqrt(jnp.sum(diagonal, axis=1, keepdims=True)), row

    def scaled():
        column, row = scales()
        a_ref[...] = s_ref[...] * column * row

    def square():
        r = r_ref[...].astype(BF16)
        t = dot(r, r)
        t_ref[...] = t
        return jnp.sum(t * t)

    def residual():
        dot_full(r_ref, a_ref, x_ref)
        r_ref[...] = eye(width).astype(F32) - r_ref[...]

    scaled()
    one = eye(width).astype(F32)
    e = one - a_ref[...]
    e1 = e.astype(BF16)
    e2 = dot(e1, e1).astype(BF16)
    x = one + e
    x_ref[...] = x + dot(x.astype(BF16), e2)
    r_ref[...] = one - dot_split(split(a_ref[...]), split(x_ref[...]))
    norm = square()
    hard = jnp.logical_not(norm <= RESIDUAL**2)
    if known_hard is not None:
        hard = jnp.logical_or(hard, known_hard)

    @pl.when(hard)
    def _():
        if refresh is not None:
            refresh()
        scaled()

        @pl.when(jnp.logical_not(norm < 0.25))
        def _():
            largest = jnp.max(jnp.sum(jnp.abs(a_ref[...]), axis=1, keepdims=True))
            x_ref[...] = jnp.where(eye(width), 1.0 / largest, 0.0)

        residual()

        def far(state):
            return jnp.logical_and(state[0] < STEPS, state[1] > 0.01 * RESIDUAL**2)

        def newton(state):
            dot_full(t_ref, x_ref, r_ref)
            x_ref[...] += t_ref[...]
            residual()
            return state[0] + 1, square()

        lax.while_loop(far, newton, (jnp.int32(0), square()))

    step = (r_ref[...] + t_ref[...]).astype(BF16)
    column, row = scales()
    x_ref[...] = (x_ref[...] + dot(x_ref[...].astype(BF16), step)) * column * row
    return hard


def part(ref, i, start, rows, blocks, count):
    at = i * (blocks * LANES + HALF) + start
    return ref[at : at + rows] * (1.0 / count)


def put(ref, i, j, block):
    ref[i * LANES : (i + 1) * LANES, j * LANES : (j + 1) * LANES] = block


def put_diagonal(ref, slabs_ref, damp, count):
    blocks = ref.shape[0] // LANES
    unit = eye(LANES)
    for i in range(blocks):
        put(ref, i, i, part(slabs_ref, i, 0, LANES, blocks, count) + jnp.where(unit, damp, 0.0))
        for j in range(i + 1, blocks):
            block = part(slabs_ref, i, (j - i) * LANES, LANES, blocks, count)
            put(ref, i, j, block)
            put(ref, j, i, block.T)


def first_kernel(count, damp_ref, mine_ref, x_ref, hard_ref, s_ref, a_ref, r_ref, t_ref):
    put_diagonal(s_ref, mine_ref, damp_ref[0], count)
    hard_ref[0] = invert(s_ref, a_ref, x_ref, r_ref, t_ref).astype(jnp.int32)


def solve_kernel(
    count, core_ref, hard_ref, damp_ref, damp_other_ref, mine_ref, theirs_ref, first_ref, own_ref,
    other_ref, solved_ref, score_ref, s_ref, d_ref, c_ref, ct_ref, a_ref, x_ref, r_ref, t_ref, y_ref,
    left_ref,
):
    near = core_ref[0] == 0
    width = own_ref.shape[1]
    blocks = width // LANES
    damp, damp_other = damp_ref[0], damp_other_ref[0]

    for i in range(blocks):
        for j in range(i):
            start = (j + blocks - i) * LANES
            block = part(mine_ref, i, start, LANES, blocks, count)
            put(c_ref, i, j, block)
            put(ct_ref, j, i, block.T)
            block = part(theirs_ref, i, start, LANES, blocks, count)
            put(ct_ref, i, j, block)
            put(c_ref, j, i, block.T)
        mine = part(mine_ref, i, blocks * LANES, HALF, blocks, count)
        theirs = part(theirs_ref, i, blocks * LANES, HALF, blocks, count)
        block = jnp.concatenate([jnp.where(near, mine, theirs), jnp.where(near, theirs, mine)], 0)
        turned = block.T
        put(c_ref, i, i, jnp.where(near, block, turned))
        put(ct_ref, i, i, jnp.where(near, turned, block))
    put_diagonal(d_ref, theirs_ref, damp_other, count)

    first = split(first_ref[...])
    y_ref[...] = dot_split(first, split(c_ref[...]))
    s_ref[...] = d_ref[...] - dot_split(split(ct_ref[...]), split(y_ref[...]))

    def refresh():
        dot_full(y_ref, first_ref, c_ref)
        dot_full(s_ref, ct_ref, y_ref, d_ref)

    hard = invert(s_ref, a_ref, x_ref, r_ref, t_ref, refresh, hard_ref[0] > 0)

    def outputs(z_own, z_other):
        solved_ref[...] = z_own
        gain = own_ref[...].astype(F32) * z_own + other_ref[...].astype(F32) * z_other
        penalty = damp * (z_own * z_own) + damp_other * (z_other * z_other)

        def candidate_sum(terms):
            folded = terms[:, :LANES]
            for b in range(1, blocks):
                folded = folded + terms[:, b * LANES : (b + 1) * LANES]
            return jnp.sum(folded.T, axis=0, keepdims=True)

        gain, penalty = candidate_sum(gain), candidate_sum(penalty)
        score_ref[...] = (gain - penalty) / (1.0 + gain)

    @pl.when(hard)
    def _():
        count_rows = left_ref.shape[0]
        top, bottom = pl.ds(0, count_rows), pl.ds(count_rows, count_rows)
        z_own, z_other = a_ref.at[top], a_ref.at[bottom]
        rest_own, rest_other = r_ref.at[top], r_ref.at[bottom]
        step_own, step_other = t_ref.at[top], t_ref.at[bottom]
        put_diagonal(s_ref, mine_ref, damp, count)
        a_ref[...] = jnp.zeros_like(a_ref)
        rest_own[...] = own_ref[...].astype(F32)
        rest_other[...] = other_ref[...].astype(F32)

        def refine(_, carry):
            dot_full(left_ref, rest_own, y_ref, rest_other)
            dot_full(step_other, left_ref, x_ref)
            dot_full(left_ref, rest_own, first_ref)
            dot_full(step_own, step_other, y_ref, left_ref, ((1,), (1,)))
            a_ref[...] += t_ref[...]
            dot_full(left_ref, z_own, s_ref, own_ref)
            dot_full(rest_own, z_other, ct_ref, left_ref)
            dot_full(left_ref, z_own, c_ref, other_ref)
            dot_full(rest_other, z_other, d_ref, left_ref)
            return carry

        lax.fori_loop(0, REFINEMENTS, refine, 0)
        outputs(z_own[...], z_other[...])

    @pl.when(jnp.logical_not(hard))
    def _():
        own = (own_ref[...],)
        y = split(y_ref[...])
        left = other_ref[...].astype(F32) - dot_split(own, y)
        z_other = dot_split(split(left), split(x_ref[...]))
        z_own = dot_split(own, split(first_ref[...])) - dot_split(split(z_other), y, ((1,), (1,)))
        outputs(z_own, z_other)


SMEM = pl.BlockSpec(memory_space=pltpu.SMEM)
VMEM = pl.BlockSpec(memory_space=pltpu.VMEM)


def call(kernel, out_shape, in_specs, mebibytes, megaflops=0, out_specs=VMEM, scratch=()):
    return pl.pallas_call(
        kernel,
        out_shape=out_shape,
        in_specs=in_specs,
        out_specs=out_specs,
        scratch_shapes=scratch,
        compiler_params=pltpu.CompilerParams(vmem_limit_bytes=mebibytes * 2**20),
        cost_estimate=pl.CostEstimate(
            flops=megaflops * 10**6, bytes_accessed=2**20, transcendentals=0
        ),
    )


def exchanged(array, axis):
    devices = lax.axis_size(axis)
    parts = lax.all_to_all(array.reshape(devices, 1, -1), axis, 0, 0, tiled=True)
    return parts.reshape(array.shape)


def from_others(array, axis):
    devices = lax.axis_size(axis)
    return [
        lax.ppermute(array, axis, [(i, (i + shift) % devices) for i in range(devices)])
        for shift in range(1, devices)
    ]


def on_device(grads, labeled, damping):
    _, row_count, width = grads.shape
    count = row_count * lax.axis_size(EX)
    core = lax.axis_index("layer").astype(jnp.int32).reshape(1)
    swap = [(0, 1), (1, 0)]
    own = grads[0]
    labeled = labeled.reshape(1, row_count)
    other = lax.ppermute(own, "layer", swap)
    damping_other = lax.ppermute(damping, "layer", swap)
    blocks = width // LANES
    rows = blocks * (blocks * LANES + HALF)
    pieces, planes = lax.axis_size(NEAR), lax.axis_size(FAR)
    square = pltpu.VMEM((width, width), F32)
    matrix = jax.ShapeDtypeStruct((width, width), F32)

    def slabs(length):
        return jax.ShapeDtypeStruct((length, LANES), F32)

    own_t = call(mask_kernel, jax.ShapeDtypeStruct((width, row_count), BF16), [VMEM] * 2, 8, 500)(
        labeled, own
    )
    products = call(gram_kernel, slabs(rows), [SMEM] + [VMEM] * 4, 16, 500)(
        core, labeled, own_t, own, other
    )
    partial = call(sum_kernel, slabs(rows // pieces), [VMEM], 8, 50)(exchanged(products, NEAR))
    partials = [partial, *from_others(partial, FAR)]
    total = call(total_kernel, slabs(rows), [VMEM] * planes, 8, 50)(*partials)
    mine = exchanged(total, NEAR)
    theirs = lax.ppermute(mine, "layer", swap)
    first, hard = call(
        functools.partial(first_kernel, count),
        (matrix, jax.ShapeDtypeStruct((1,), jnp.int32)),
        [SMEM, VMEM],
        16,
        3000,
        (VMEM, SMEM),
        [square] * 4,
    )(damping, mine)
    solved, score = call(
        functools.partial(solve_kernel, count),
        (
            jax.ShapeDtypeStruct((row_count, width), F32),
            jax.ShapeDtypeStruct((1, row_count), F32),
        ),
        [SMEM] * 4 + [VMEM] * 5,
        32,
        6000,
        (VMEM, VMEM),
        [square] * 9 + [pltpu.VMEM((row_count, width), F32)],
    )(core, hard, damping, damping_other, mine, theirs, first, own, other)
    return solved[None], score.reshape(row_count)


def solution(mesh):
    torus = Mesh(mesh.devices.reshape(mesh.shape["layer"], 4, 2, 4, 4), ("layer", *EX))
    in_specs = (P("layer", EX, None), P(EX), P("layer"))
    out_specs = (P("layer", EX, None), P(EX))
    return jax.shard_map(
        on_device, mesh=torus, in_specs=in_specs, out_specs=out_specs, check_vma=False
    )
```

time: 177 us -> 257 us (1.45)
  Pallas kernels: 104 us -> 190 us
  blocking collectives: 63.8 us -> 48.2 us
  starting transfers between devices: 0.6 us -> 9.9 us
    pallas_call x4 -> x6, Pallas kernels: 104 us -> 190 us  [the longest x1 127 us: on_device(): call(functools.partial(solve_kernel, count), (jax.ShapeDtypeStruct((row_c...]
    all_to_all x3 -> x2, blocking collectives: 63.8 us -> 48.2 us  [exchanged(): lax.all_to_all(array.reshape(devices, 1, -1), axis, 0, 0, tiled=True)]
    ppermute x1 -> x4, starting transfers between devices: 0.51 us -> 9.8 us  [the longest x3 9.29 us: from_others(): lax.ppermute(array, axis, [(i, (i + shift) % devices) for i in range(devi...]
  transfers between devices with their start and end apart: 3 -> 6, of which waited for: 2 -> 1; matrix products, arithmetic and copies ran while one was open for 0% -> 0% of each run, Pallas kernels for 0% -> 25%
where the time goes in v5:
time: 257 us; the launch traced here: 256 us
  Pallas kernels  190 us (74%)
  blocking collectives  48.2 us (19%)
  starting transfers between devices  9.9 us (4%)
  waiting for transfers between devices  4.11 us (2%)
    pallas_call x1, Pallas kernels, on_device(): call(functools.partial(solve_kernel, count), (jax.ShapeDtypeStruct((row_c...  127 us
    pallas_call x1, Pallas kernels, on_device(): call(functools.partial(first_kernel, count), (matrix, jax.ShapeDtypeStruc...  62.8 us
    all_to_all x2, blocking collectives, exchanged(): lax.all_to_all(array.reshape(devices, 1, -1), axis, 0, 0, tiled=True)  48.2 us
    ppermute x3, starting transfers between devices, from_others(): lax.ppermute(array, axis, [(i, (i + shift) % devices) for i in range(devi...  9.29 us
  transfers between devices with their start and end apart: 6, of which 1 were waited for; matrix products, arithmetic and copies ran while one was open for 0% of the time, Pallas kernels for 25%

profile of v5, /device:TPU:8, one launch (start us, length us, event | category | flops | bytes accessed | tf_op | source)
XLA Modules:
  0.0 256.2 jit_solution(1307837948438868917)
XLA Ops:
  0.6 0.1 collective-permute-start
  0.7 0.0 copy-start
  0.8 0.9 copy-done
  1.7 0.7 copy-done.2
  2.4 0.1 shard_map.50.own_t_ref
  2.5 0.0 collective-permute-done.other_ref
  2.5 0.8 copy-done.1
  3.3 0.4 shard_map.51
  3.7 27.2 %all_to_all.10 = f32[32,1,9216]{2,1,0:T(1,128)S(1)} all-to-all(f32[32,1,9216]{2,1,0:T(1,128)S(1)} %bitcast.10), channel_id=1, replica_groups=mesh['layer'=2,'z_hi'=4,'z_lo'=2,'y'=4,'x'=4] {'z_lo','y','x'}, dimensions={0} | all-to-all | bytes 2359296 | tf_op jit(solution)/shard_map/all_to_all | solution.py:298
  31.0 0.1 shard_map.52.refs_0_
  31.1 5.5 %collective-permute-start.3 = (f32[72,128]{1,0:T(8,128)S(1)}, f32[72,128]{1,0:T(8,128)S(1)}, u32[]{:S(2)}, u32[]{:S(2)}) collective-permute-start(f32[72,128]{1,0:T(8,128)S(1)} %shard_map.52.refs_0_), channel_id=1, source_target_pairs={{0,96},{32,0},{64,32},{96,64},{1,97},{33,1},{65,33},{97,65},{2,98}... | collective-permute-start | bytes 110600 | tf_op jit(solution)/shard_map/ppermute | solution.py:305
  36.5 1.4 collective-permute-start.2
  38.0 2.4 collective-permute-start.1
  40.4 0.0 collective-permute-done.3.refs_3_
  40.4 4.1 %collective-permute-done.2.refs_2_ = f32[72,128]{1,0:T(8,128)S(1)} collective-permute-done((f32[72,128]{1,0:T(8,128)S(1)}, f32[72,128]{1,0:T(8,128)S(1)}, u32[]{:S(2)}, u32[]{:S(2)}) %collective-permute-start.2) | collective-permute-done | bytes 36896 | tf_op jit(solution)/shard_map/ppermute | solution.py:305
  44.4 0.0 collective-permute-done.1.refs_1_
  44.5 0.1 shard_map.53
  44.5 21.0 %all_to_all.11 = f32[32,1,9216]{2,1,0:T(1,128)S(1)} all-to-all(f32[32,1,9216]{2,1,0:T(1,128)S(1)} %bitcast.9), channel_id=1, replica_groups=mesh['layer'=2,'z_hi'=4,'z_lo'=2,'y'=4,'x'=4] {'z_lo','y','x'}, dimensions={0} | all-to-all | bytes 2359296 | tf_op jit(solution)/shard_map/all_to_all | solution.py:298
  65.5 0.0 collective-permute-start.5
  65.6 0.5 collective-permute-start.4
  66.7 62.8 %shard_map.54 = (f32[512,512]{1,0:T(8,128)S(1)}, s32[1]{0:T(128)}) custom-call(f32[1]{0:T(128)S(6)} %copy.7.damp_ref, f32[2304,128]{1,0:T(8,128)S(1)} %bitcast.13), custom_call_target="tpu_custom_call" | custom-call | flops 3000000000 | bytes 1048576 | tf_op jit(solution)/shard_map/pallas_call | solution.py:339
  129.5 0.0 collective-permute-done.4.damp_other_ref
  129.5 0.0 collective-permute-done.5.theirs_ref
  129.5 126.7 %shard_map.55 = (f32[256,512]{1,0:T(8,128)}, f32[1,256]{1,0:T(1,128)}) custom-call(s32[1]{0:T(128)} %bitcast.core_ref, s32[1]{0:T(128)} %get-tuple-element.6.hard_ref, f32[1]{0:T(128)S(6)} %copy.7.damp_ref, f32[1]{0:T(128)} %collective-permute-done.4.damp_other_ref, f32[2304,128]{1,0:T(8,128)S(1)} %bitcast.14, ...), custom_call_target="tpu_custom_call" | custom-call | flops 6000000000 | bytes 1048576 | tf_op jit(solution)/shard_map/pallas_call | solution.py:348
  (4 shorter events, 0.0 us)
Async XLA Ops:
  0.6 1.9 copy-start.3
  0.6 1.9 collective-permute-start
  0.7 1.0 copy-start
  1.7 0.7 copy-start.2
  2.4 0.9 copy-start.1
  31.1 9.3 %collective-permute-start.3 = (f32[72,128]{1,0:T(8,128)S(1)}, f32[72,128]{1,0:T(8,128)S(1)}, u32[]{:S(2)}, u32[]{:S(2)}) collective-permute-start(f32[72,128]{1,0:T(8,128)S(1)} %shard_map.52.refs_0_), channel_id=1, source_target_pairs={{0,96},{32,0},{64,32},{96,64},{1,97},{33,1},{65,33},{97,65},{2,98}... | collective-permute-start | bytes 110600 | tf_op jit(solution)/shard_map/ppermute | solution.py:305
  36.5 7.9 %collective-permute-start.2 = (f32[72,128]{1,0:T(8,128)S(1)}, f32[72,128]{1,0:T(8,128)S(1)}, u32[]{:S(2)}, u32[]{:S(2)}) collective-permute-start(f32[72,128]{1,0:T(8,128)S(1)} %shard_map.52.refs_0_), channel_id=1, source_target_pairs={{0,64},{32,96},{64,0},{96,32},{1,65},{33,97},{65,1},{97,33},{2,66}... | collective-permute-start | bytes 110600 | tf_op jit(solution)/shard_map/ppermute | solution.py:305
  38.0 6.5 %collective-permute-start.1 = (f32[72,128]{1,0:T(8,128)S(1)}, f32[72,128]{1,0:T(8,128)S(1)}, u32[]{:S(2)}, u32[]{:S(2)}) collective-permute-start(f32[72,128]{1,0:T(8,128)S(1)} %shard_map.52.refs_0_), channel_id=1, source_target_pairs={{0,32},{32,64},{64,96},{96,0},{1,33},{33,65},{65,97},{97,1},{2,34}... | collective-permute-start | bytes 110600 | tf_op jit(solution)/shard_map/ppermute | solution.py:305
  65.5 64.0 %collective-permute-start.5 = (f32[2304,128]{1,0:T(8,128)S(1)}, f32[2304,128]{1,0:T(8,128)S(1)}, u32[]{:S(2)}, u32[]{:S(2)}) collective-permute-start(f32[2304,128]{1,0:T(8,128)S(1)} %bitcast.12), channel_id=1, source_target_pairs={{0,128},{128,0},{1,129},{129,1},{2,130},{130,2},{3,131},{131,3},{4... | collective-permute-start | bytes 3538952 | tf_op jit(solution)/shard_map/ppermute | solution.py:338
  65.6 64.0 %collective-permute-start.4 = (f32[1]{0:T(128)}, f32[1]{0:T(128)}, u32[]{:S(2)}, u32[]{:S(2)}) collective-permute-start(f32[1]{0:T(128)} %param.5), channel_id=1, source_target_pairs={{0,128},{128,0},{1,129},{129,1},{2,130},{130,2},{3,131},{131,3},{4... | collective-permute-start | bytes 20 | tf_op jit(solution)/shard_map/ppermute | solution.py:318

commit v6 on v5

--- a/solution.py
+++ b/solution.py
@@ -9,7 +9,7 @@
 from jax.sharding import PartitionSpec as P
 
 EX = ("z_hi", "z_lo", "y", "x")
-FAR, NEAR = EX[0], EX[1:]
+FAR, PAIR, SHEET, NEAR = EX[0], EX[1], EX[2:], EX[1:]
 F32, BF16 = jnp.float32, jnp.bfloat16
 LANES = 128
 HALF = LANES // 2
@@ -49,29 +49,41 @@
     lax.fori_loop(0, TILES, step, 0)
 
 
-def mask_kernel(labeled_ref, own_ref, out_ref):
-    keep = (labeled_ref[...] > 0).astype(F32)
-    out_ref[...] = (own_ref[...].astype(F32).T * keep).astype(BF16)
-
-
-def gram_kernel(core_ref, labeled_ref, own_t_ref, own_ref, other_ref, out_ref):
-    core = core_ref[0]
-    keep = (labeled_ref[...] > 0).astype(F32)
-    own_t, own, other = own_t_ref[...], own_ref[...], other_ref[...]
-    blocks = own.shape[1] // LANES
-    first_t = jnp.where(core == 0, own_t, (other.astype(F32).T * keep).astype(BF16))
-    last = jnp.where(core == 0, other, own)
-    both = jnp.concatenate([own, other], axis=1)
+def masked_turned(rows, labeled):
+    return (rows.astype(F32).T * (labeled > 0).astype(F32)).astype(BF16)
+
+
+def mask_kernel(labeled_ref, own_ref, other_ref, own_t_ref, other_t_ref):
+    own_t_ref[...] = masked_turned(own_ref[...], labeled_ref[...])
+    other_t_ref[...] = masked_turned(other_ref[...], labeled_ref[...])
+
+
+def gram_kernel(
+    place_ref, _, labeled_ref, own_t_ref, other_t_ref, pair_ref, pair_other_ref, out_ref, turned_ref
+):
+    core, side = place_ref[0], place_ref[1]
+    width, rows = own_t_ref.shape
+    blocks = width // LANES
+    turned_ref[:width, :rows] = own_t_ref[...]
+    turned_ref[width:, :rows] = other_t_ref[...]
+    turned_ref[:width, rows:] = masked_turned(pair_ref[...], labeled_ref[...])
+    turned_ref[width:, rows:] = masked_turned(pair_other_ref[...], labeled_ref[...])
     slab = blocks * LANES + HALF
-    for i in range(blocks):
-        rows = own_t[i * LANES : (i + 1) * LANES]
-        product = dot(rows, both[:, i * LANES : (i + blocks) * LANES])
+    across = ((1,), (1,))
+
+    def at(start, size):
+        return turned_ref[pl.ds(pl.multiple_of(start, HALF), size), :]
+
+    for k in range(blocks // 2):
+        start = (side * (blocks // 2) + k) * LANES
+        product = dot(at(start, LANES), at(start, width), across)
         for b in range(blocks):
-            start = i * slab + b * LANES
-            out_ref[start : start + LANES] = product[:, b * LANES : (b + 1) * LANES]
-        middle = dot(first_t[i * LANES : (i + 1) * LANES], last[:, i * LANES : (i + 1) * LANES])
-        start = i * slab + blocks * LANES
-        out_ref[start : start + HALF] = jnp.where(core == 0, middle[:HALF], middle[HALF:])
+            out = k * slab + b * LANES
+            out_ref[out : out + LANES] = product[:, b * LANES : (b + 1) * LANES]
+        layer = core * width
+        middle = dot(at(start + layer + core * HALF, HALF), at(start + width - layer, LANES), across)
+        out = k * slab + blocks * LANES
+        out_ref[out : out + HALF] = middle
 
 
 def sum_kernel(in_ref, out_ref):
@@ -311,27 +323,41 @@
     _, row_count, width = grads.shape
     count = row_count * lax.axis_size(EX)
     core = lax.axis_index("layer").astype(jnp.int32).reshape(1)
+    side = lax.axis_index(PAIR).astype(jnp.int32).reshape(1)
     swap = [(0, 1), (1, 0)]
     own = grads[0]
     labeled = labeled.reshape(1, row_count)
+    pair = lax.ppermute(own, PAIR, swap)
+    labeled_pair = lax.ppermute(labeled, PAIR, swap)
     other = lax.ppermute(own, "layer", swap)
     damping_other = lax.ppermute(damping, "layer", swap)
     blocks = width // LANES
     rows = blocks * (blocks * LANES + HALF)
-    pieces, planes = lax.axis_size(NEAR), lax.axis_size(FAR)
+    planes = lax.axis_size(FAR)
     square = pltpu.VMEM((width, width), F32)
     matrix = jax.ShapeDtypeStruct((width, width), F32)
+    turned = jax.ShapeDtypeStruct((width, row_count), BF16)
 
     def slabs(length):
         return jax.ShapeDtypeStruct((length, LANES), F32)
 
-    own_t = call(mask_kernel, jax.ShapeDtypeStruct((width, row_count), BF16), [VMEM] * 2, 8, 500)(
-        labeled, own
+    own_t, other_t = call(mask_kernel, (turned, turned), [VMEM] * 3, 8, 2000, (VMEM, VMEM))(
+        labeled, own, other
     )
-    products = call(gram_kernel, slabs(rows), [SMEM] + [VMEM] * 4, 16, 500)(
-        core, labeled, own_t, own, other
+    pair, own_t, other_t = lax.optimization_barrier((pair, own_t, other_t))
+    pair_other = lax.ppermute(pair, "layer", swap)
+    products = call(
+        gram_kernel,
+        slabs(rows // 2),
+        [SMEM] * 2 + [VMEM] * 5,
+        16,
+        500,
+        scratch=[pltpu.VMEM((2 * width, 2 * row_count), BF16)],
+    )(
+        jnp.concatenate([core, side]), damping_other, labeled_pair, own_t, other_t, pair, pair_other
     )
-    partial = call(sum_kernel, slabs(rows // pieces), [VMEM], 8, 50)(exchanged(products, NEAR))
+    sheet = exchanged(products, SHEET)
+    partial = call(sum_kernel, slabs(rows // lax.axis_size(NEAR)), [VMEM], 8, 50)(sheet)
     partials = [partial, *from_others(partial, FAR)]
     total = call(total_kernel, slabs(rows), [VMEM] * planes, 8, 50)(*partials)
     mine = exchanged(total, NEAR)

time: 257 us -> 259 us (level)
  blocking collectives: 48.2 us -> 37.6 us
  waiting for transfers between devices: 4.11 us -> 11.4 us
  starting transfers between devices: 9.9 us -> 14 us
    all_to_all x2, blocking collectives: 48.2 us -> 37.6 us  [exchanged(): lax.all_to_all(array.reshape(devices, 1, -1), axis, 0, 0, tiled=True)]
    ppermute x0 -> x3, waiting for transfers between devices: none -> 5.98 us  [the longest x1 5.21 us: on_device(): pair = lax.ppermute(own, PAIR, swap)]
    ppermute x0 -> x3, starting transfers between devices: none -> 3.75 us  [the longest x1 2 us: on_device(): pair = lax.ppermute(own, PAIR, swap)]
  transfers between devices with their start and end apart: 6 -> 9, of which waited for: 1 -> 4; matrix products, arithmetic and copies ran while one was open for 0% -> 0% of each run, Pallas kernels for 25% -> 25%
where the time goes in v6:
time: 259 us; the launch traced here: 258 us
  Pallas kernels  192 us (74%)
  blocking collectives  37.6 us (15%)
  starting transfers between devices  14 us (5%)
  waiting for transfers between devices  11.4 us (4%)
    pallas_call x1, Pallas kernels, on_device(): call(functools.partial(solve_kernel, count), (jax.ShapeDtypeStruct((row_c...  127 us
    pallas_call x1, Pallas kernels, on_device(): call(functools.partial(first_kernel, count), (matrix, jax.ShapeDtypeStruc...  62.5 us
    all_to_all x2, blocking collectives, exchanged(): lax.all_to_all(array.reshape(devices, 1, -1), axis, 0, 0, tiled=True)  37.6 us
    ppermute x3, starting transfers between devices, from_others(): lax.ppermute(array, axis, [(i, (i + shift) % devices) for i in range(devi...  9.91 us
    ppermute x1, waiting for transfers between devices, on_device(): pair = lax.ppermute(own, PAIR, swap)  5.21 us
  transfers between devices with their start and end apart: 9, of which 4 were waited for; matrix products, arithmetic and copies ran while one was open for 0% of the time, Pallas kernels for 25%

profile of v6, /device:TPU:8, one launch (start us, length us, event | category | flops | bytes accessed | tf_op | source)
XLA Modules:
  0.0 257.7 jit_solution(801356200703730932)
XLA Ops:
  0.6 0.1 collective-permute-start.3
  0.7 2.0 collective-permute-start.2
  2.7 0.0 collective-permute-done.3.other_ref
  2.7 1.0 copy-done
  3.7 0.9 shard_map.50
  4.6 5.2 %collective-permute-done.2.pair_ref = bf16[256,512]{1,0:T(8,128)(2,1)S(1)} collective-permute-done((bf16[256,512]{1,0:T(8,128)(2,1)}, bf16[256,512]{1,0:T(8,128)(2,1)S(1)}, u32[]{:S(2)}, u32[]{:S(2)}) %collective-permute-start.2) | collective-permute-done | bytes 262176 | tf_op jit(solution)/shard_map/ppermute | solution.py:330
  9.8 1.7 collective-permute-start.1
  11.6 0.2 collective-permute-start
  11.8 0.1 pad_add_fusion.place_ref
  11.9 1.0 collective-permute-done._.damp_other_ref
  12.8 0.8 collective-permute-done.1.labeled_ref
  13.6 0.0 collective-permute-done.4.pair_other_ref
  13.6 1.9 shard_map.51
  15.5 17.7 %all_to_all.10 = f32[16,1,9216]{2,1,0:T(1,128)S(1)} all-to-all(f32[16,1,9216]{2,1,0:T(1,128)S(1)} %bitcast.15), channel_id=1, replica_groups=mesh['layer'=2,'z_hi'=4,'z_lo'=2,'y'=4,'x'=4] {'y','x'}, dimensions={0} | all-to-all | bytes 1179648 | tf_op jit(solution)/shard_map/all_to_all | solution.py:310
  33.3 6.1 %collective-permute-start.7 = (f32[72,128]{1,0:T(8,128)S(1)}, f32[72,128]{1,0:T(8,128)S(1)}, u32[]{:S(2)}, u32[]{:S(2)}) collective-permute-start(f32[72,128]{1,0:T(8,128)S(1)} %shard_map.52.refs_0_), channel_id=1, source_target_pairs={{0,96},{32,0},{64,32},{96,64},{1,97},{33,1},{65,33},{97,65},{2,98}... | collective-permute-start | bytes 110600 | tf_op jit(solution)/shard_map/ppermute | solution.py:317
  39.3 1.0 collective-permute-start.6
  40.3 2.8 %collective-permute-start.5 = (f32[72,128]{1,0:T(8,128)S(1)}, f32[72,128]{1,0:T(8,128)S(1)}, u32[]{:S(2)}, u32[]{:S(2)}) collective-permute-start(f32[72,128]{1,0:T(8,128)S(1)} %shard_map.52.refs_0_), channel_id=1, source_target_pairs={{0,32},{32,64},{64,96},{96,0},{1,33},{33,65},{65,97},{97,1},{2,34}... | collective-permute-start | bytes 110600 | tf_op jit(solution)/shard_map/ppermute | solution.py:317
  43.2 0.0 collective-permute-done.7.refs_3_
  43.2 4.4 %collective-permute-done.6.refs_2_ = f32[72,128]{1,0:T(8,128)S(1)} collective-permute-done((f32[72,128]{1,0:T(8,128)S(1)}, f32[72,128]{1,0:T(8,128)S(1)}, u32[]{:S(2)}, u32[]{:S(2)}) %collective-permute-start.6) | collective-permute-done | bytes 36896 | tf_op jit(solution)/shard_map/ppermute | solution.py:317
  47.6 0.1 shard_map.53
  47.7 19.9 %all_to_all.11 = f32[32,1,9216]{2,1,0:T(1,128)S(1)} all-to-all(f32[32,1,9216]{2,1,0:T(1,128)S(1)} %bitcast.10), channel_id=1, replica_groups=mesh['layer'=2,'z_hi'=4,'z_lo'=2,'y'=4,'x'=4] {'z_lo','y','x'}, dimensions={0} | all-to-all | bytes 2359296 | tf_op jit(solution)/shard_map/all_to_all | solution.py:310
  68.3 0.0 copy-start.1
  68.3 62.5 %shard_map.54 = (f32[512,512]{1,0:T(8,128)S(1)}, s32[1]{0:T(128)}) custom-call(f32[1]{0:T(128)S(6)} %copy.7.damp_ref, f32[2304,128]{1,0:T(8,128)S(1)} %bitcast.13), custom_call_target="tpu_custom_call" | custom-call | flops 3000000000 | bytes 1048576 | tf_op jit(solution)/shard_map/pallas_call | solution.py:365
  130.8 126.9 %shard_map.55 = (f32[256,512]{1,0:T(8,128)}, f32[1,256]{1,0:T(1,128)}) custom-call(s32[1]{0:T(128)} %bitcast.core_ref, s32[1]{0:T(128)} %get-tuple-element.16.hard_ref, f32[1]{0:T(128)S(6)} %copy.7.damp_ref, f32[1]{0:T(128)} %collective-permute-done._.damp_other_ref, f32[2304,128]{1,0:T(8,128)S(1)} %bitcast.14, ...), custom_call_target="tpu_custom_call" | custom-call | flops 6000000000 | bytes 1048576 | tf_op jit(solution)/shard_map/pallas_call | solution.py:374
  (7 shorter events, 0.0 us)
Async XLA Ops:
  0.6 2.1 collective-permute-start.3
  0.7 9.1 %collective-permute-start.2 = (bf16[256,512]{1,0:T(8,128)(2,1)}, bf16[256,512]{1,0:T(8,128)(2,1)S(1)}, u32[]{:S(2)}, u32[]{:S(2)}) collective-permute-start(bf16[256,512]{1,0:T(8,128)(2,1)} %bitcast.17), channel_id=1, source_target_pairs={{0,16},{16,0},{1,17},{17,1},{2,18},{18,2},{3,19},{19,3},{4,20},{20... | collective-permute-start | bytes 786440 | tf_op jit(solution)/shard_map/ppermute | solution.py:330
  2.7 1.0 copy-start
  9.8 3.8 %collective-permute-start.4 = (bf16[256,512]{1,0:T(8,128)(2,1)S(1)}, bf16[256,512]{1,0:T(8,128)(2,1)S(1)}, u32[]{:S(2)}, u32[]{:S(2)}) collective-permute-start(bf16[256,512]{1,0:T(8,128)(2,1)S(1)} %collective-permute-done.2.pair_ref), channel_id=1, source_target_pairs={{0,128},{128,0},{1,129},{129,1},{2,130},{130,2},{3,131},{131,3},{4... | collective-permute-start | bytes 786440 | tf_op jit(solution)/shard_map/ppermute | solution.py:348
  9.8 3.8 %collective-permute-start.1 = (s32[1,256]{1,0:T(1,128)}, s32[1,256]{1,0:T(1,128)S(1)}, u32[]{:S(2)}, u32[]{:S(2)}) collective-permute-start(s32[1,256]{1,0:T(1,128)} %bitcast.2.labeled_ref), channel_id=1, source_target_pairs={{0,16},{16,0},{1,17},{17,1},{2,18},{18,2},{3,19},{19,3},{4,20},{20... | collective-permute-start | bytes 3080 | tf_op jit(solution)/shard_map/ppermute | solution.py:331
  11.6 1.3 collective-permute-start
  33.3 9.9 %collective-permute-start.7 = (f32[72,128]{1,0:T(8,128)S(1)}, f32[72,128]{1,0:T(8,128)S(1)}, u32[]{:S(2)}, u32[]{:S(2)}) collective-permute-start(f32[72,128]{1,0:T(8,128)S(1)} %shard_map.52.refs_0_), channel_id=1, source_target_pairs={{0,96},{32,0},{64,32},{96,64},{1,97},{33,1},{65,33},{97,65},{2,98}... | collective-permute-start | bytes 110600 | tf_op jit(solution)/shard_map/ppermute | solution.py:317
  39.3 8.3 %collective-permute-start.6 = (f32[72,128]{1,0:T(8,128)S(1)}, f32[72,128]{1,0:T(8,128)S(1)}, u32[]{:S(2)}, u32[]{:S(2)}) collective-permute-start(f32[72,128]{1,0:T(8,128)S(1)} %shard_map.52.refs_0_), channel_id=1, source_target_pairs={{0,64},{32,96},{64,0},{96,32},{1,65},{33,97},{65,1},{97,33},{2,66}... | collective-permute-start | bytes 110600 | tf_op jit(solution)/shard_map/ppermute | solution.py:317
  40.3 7.3 %collective-permute-start.5 = (f32[72,128]{1,0:T(8,128)S(1)}, f32[72,128]{1,0:T(8,128)S(1)}, u32[]{:S(2)}, u32[]{:S(2)}) collective-permute-start(f32[72,128]{1,0:T(8,128)S(1)} %shard_map.52.refs_0_), channel_id=1, source_target_pairs={{0,32},{32,64},{64,96},{96,0},{1,33},{33,65},{65,97},{97,1},{2,34}... | collective-permute-start | bytes 110600 | tf_op jit(solution)/shard_map/ppermute | solution.py:317
  67.6 63.2 %collective-permute-start.8 = (f32[2304,128]{1,0:T(8,128)S(1)}, f32[2304,128]{1,0:T(8,128)S(1)}, u32[]{:S(2)}, u32[]{:S(2)}) collective-permute-start(f32[2304,128]{1,0:T(8,128)S(1)} %bitcast.12), channel_id=1, source_target_pairs={{0,128},{128,0},{1,129},{129,1},{2,130},{130,2},{3,131},{131,3},{4... | collective-permute-start | bytes 3538952 | tf_op jit(solution)/shard_map/ppermute | solution.py:364
  68.3 62.6 %copy-start.1 = (bf16[1,256,512]{2,1,0:T(8,128)(2,1)S(1)}, bf16[1,256,512]{2,1,0:T(8,128)(2,1)}, u32[]{:S(2)}) copy-start(bf16[1,256,512]{2,1,0:T(8,128)(2,1)} %param.3) | copy-start | bytes 786436

commit v7 on v5

--- a/solution.py
+++ b/solution.py
@@ -49,14 +49,27 @@
     lax.fori_loop(0, TILES, step, 0)
 
 
-def mask_kernel(labeled_ref, own_ref, out_ref):
+def mask_kernel(
+    damp_ref, damp_other_ref, labeled_hbm, own_hbm, own_t_ref, own_ref, keep_ref, damps_ref, labeled_ref, sems
+):
+    arriving = [
+        pltpu.make_async_copy(own_hbm, own_ref, sems.at[0]),
+        pltpu.make_async_copy(labeled_hbm, labeled_ref, sems.at[1]),
+    ]
+    for copy in arriving:
+        copy.start()
+    damps_ref[:8] = jnp.full((8, LANES), damp_ref[0])
+    damps_ref[8:] = jnp.full((8, LANES), damp_other_ref[0])
+    for copy in arriving:
+        copy.wait()
     keep = (labeled_ref[...] > 0).astype(F32)
-    out_ref[...] = (own_ref[...].astype(F32).T * keep).astype(BF16)
-
-
-def gram_kernel(core_ref, labeled_ref, own_t_ref, own_ref, other_ref, out_ref):
+    own_t_ref[...] = (own_ref[...].astype(F32).T * keep).astype(BF16)
+    keep_ref[...] = keep
+
+
+def gram_kernel(core_ref, keep_ref, own_t_ref, own_ref, other_ref, out_ref):
     core = core_ref[0]
-    keep = (labeled_ref[...] > 0).astype(F32)
+    keep = keep_ref[...]
     own_t, own, other = own_t_ref[...], own_ref[...], other_ref[...]
     blocks = own.shape[1] // LANES
     first_t = jnp.where(core == 0, own_t, (other.astype(F32).T * keep).astype(BF16))
@@ -125,8 +138,9 @@
     e1 = e.astype(BF16)
     e2 = dot(e1, e1).astype(BF16)
     x = one + e
-    x_ref[...] = x + dot(x.astype(BF16), e2)
-    r_ref[...] = one - dot_split(split(a_ref[...]), split(x_ref[...]))
+    x = (x + dot(x.astype(BF16), e2)).astype(BF16)
+    x_ref[...] = x.astype(F32)
+    r_ref[...] = one - dot_split(split(a_ref[...]), (x,))
     norm = square()
     hard = jnp.logical_not(norm <= RESIDUAL**2)
     if known_hard is not None:
@@ -183,19 +197,19 @@
 
 
 def first_kernel(count, damp_ref, mine_ref, x_ref, hard_ref, s_ref, a_ref, r_ref, t_ref):
-    put_diagonal(s_ref, mine_ref, damp_ref[0], count)
+    put_diagonal(s_ref, mine_ref, damp_ref[:1], count)
     hard_ref[0] = invert(s_ref, a_ref, x_ref, r_ref, t_ref).astype(jnp.int32)
 
 
 def solve_kernel(
-    count, core_ref, hard_ref, damp_ref, damp_other_ref, mine_ref, theirs_ref, first_ref, own_ref,
-    other_ref, solved_ref, score_ref, s_ref, d_ref, c_ref, ct_ref, a_ref, x_ref, r_ref, t_ref, y_ref,
-    left_ref,
+    count, core_ref, hard_ref, damps_ref, mine_ref, theirs_ref, first_ref, own_ref, other_ref,
+    solved_ref, score_ref, s_ref, d_ref, c_ref, ct_ref, a_ref, x_ref, r_ref, t_ref, y_ref,
+    left_ref, z_ref, sems,
 ):
     near = core_ref[0] == 0
     width = own_ref.shape[1]
     blocks = width // LANES
-    damp, damp_other = damp_ref[0], damp_other_ref[0]
+    damp, damp_other = damps_ref[:1], damps_ref[8:9]
 
     for i in range(blocks):
         for j in range(i):
@@ -224,19 +238,34 @@
 
     hard = invert(s_ref, a_ref, x_ref, r_ref, t_ref, refresh, hard_ref[0] > 0)
 
-    def outputs(z_own, z_other):
-        solved_ref[...] = z_own
-        gain = own_ref[...].astype(F32) * z_own + other_ref[...].astype(F32) * z_other
-        penalty = damp * (z_own * z_own) + damp_other * (z_other * z_other)
-
-        def candidate_sum(terms):
-            folded = terms[:, :LANES]
-            for b in range(1, blocks):
-                folded = folded + terms[:, b * LANES : (b + 1) * LANES]
-            return jnp.sum(folded.T, axis=0, keepdims=True)
-
-        gain, penalty = candidate_sum(gain), candidate_sum(penalty)
-        score_ref[...] = (gain - penalty) / (1.0 + gain)
+    half = z_ref.shape[0] // 2
+    parts = [pl.ds(0, half), pl.ds(half, half)]
+    leaving = [
+        pltpu.make_async_copy(z_ref.at[p], solved_ref.at[p], sems.at[i]) for i, p in enumerate(parts)
+    ]
+
+    def candidate_sum(terms):
+        folded = terms[:, :LANES]
+        for b in range(1, blocks):
+            folded = folded + terms[:, b * LANES : (b + 1) * LANES]
+        return jnp.sum(folded.T, axis=0, keepdims=True)
+
+    def scores(p, z_own, z_other):
+        gain = own_ref[p, :].astype(F32) * z_own + other_ref[p, :].astype(F32) * z_other
+        gain = candidate_sum(gain)
+        penalty = damp * candidate_sum(z_own * z_own) + damp_other * candidate_sum(z_other * z_other)
+        return (gain - penalty) / (1.0 + gain)
+
+    def outputs(solve_rows):
+        found = []
+        for p, copy in zip(parts, leaving):
+            z_own, z_other = solve_rows(p)
+            z_ref[p, :] = z_own
+            copy.start()
+            found.append((p, z_own, z_other))
+        score_ref[...] = jnp.concatenate([scores(*each) for each in found], axis=1)
+        for copy in leaving:
+            copy.wait()
 
     @pl.when(hard)
     def _():
@@ -263,20 +292,24 @@
             return carry
 
         lax.fori_loop(0, REFINEMENTS, refine, 0)
-        outputs(z_own[...], z_other[...])
+        outputs(lambda p: (z_own[p, :], z_other[p, :]))
 
     @pl.when(jnp.logical_not(hard))
     def _():
-        own = (own_ref[...],)
-        y = split(y_ref[...])
-        left = other_ref[...].astype(F32) - dot_split(own, y)
-        z_other = dot_split(split(left), split(x_ref[...]))
-        z_own = dot_split(own, split(first_ref[...])) - dot_split(split(z_other), y, ((1,), (1,)))
-        outputs(z_own, z_other)
+        y, x, p0 = split(y_ref[...]), split(x_ref[...]), split(first_ref[...])
+
+        def solve_rows(p):
+            own = (own_ref[p, :],)
+            left = other_ref[p, :].astype(F32) - dot_split(own, y)
+            z_other = dot_split(split(left), x)
+            return dot_split(own, p0) - dot_split(split(z_other), y, ((1,), (1,))), z_other
+
+        outputs(solve_rows)
 
 
 SMEM = pl.BlockSpec(memory_space=pltpu.SMEM)
 VMEM = pl.BlockSpec(memory_space=pltpu.VMEM)
+HBM = pl.BlockSpec(memory_space=pltpu.HBM)
 
 
 def call(kernel, out_shape, in_specs, mebibytes, megaflops=0, out_specs=VMEM, scratch=()):
@@ -325,11 +358,22 @@
     def slabs(length):
         return jax.ShapeDtypeStruct((length, LANES), F32)
 
-    own_t = call(mask_kernel, jax.ShapeDtypeStruct((width, row_count), BF16), [VMEM] * 2, 8, 500)(
-        labeled, own
-    )
+    own_t, own, keep, damps = call(
+        mask_kernel,
+        (
+            jax.ShapeDtypeStruct((width, row_count), BF16),
+            jax.ShapeDtypeStruct((row_count, width), BF16),
+            jax.ShapeDtypeStruct((1, row_count), F32),
+            jax.ShapeDtypeStruct((16, LANES), F32),
+        ),
+        [SMEM, SMEM, HBM, HBM],
+        8,
+        2000,
+        (VMEM,) * 4,
+        [pltpu.VMEM((1, row_count), jnp.int32), pltpu.SemaphoreType.DMA((2,))],
+    )(damping, damping_other, labeled, own)
     products = call(gram_kernel, slabs(rows), [SMEM] + [VMEM] * 4, 16, 500)(
-        core, labeled, own_t, own, other
+        core, keep, own_t, own, other
     )
     partial = call(sum_kernel, slabs(rows // pieces), [VMEM], 8, 50)(exchanged(products, NEAR))
     partials = [partial, *from_others(partial, FAR)]
@@ -339,24 +383,24 @@
     first, hard = call(
         functools.partial(first_kernel, count),
         (matrix, jax.ShapeDtypeStruct((1,), jnp.int32)),
-        [SMEM, VMEM],
+        [VMEM] * 2,
         16,
         3000,
         (VMEM, SMEM),
         [square] * 4,
-    )(damping, mine)
+    )(damps, mine)
     solved, score = call(
         functools.partial(solve_kernel, count),
         (
             jax.ShapeDtypeStruct((row_count, width), F32),
             jax.ShapeDtypeStruct((1, row_count), F32),
         ),
-        [SMEM] * 4 + [VMEM] * 5,
+        [SMEM] * 2 + [VMEM] * 6,
         32,
         6000,
-        (VMEM, VMEM),
-        [square] * 9 + [pltpu.VMEM((row_count, width), F32)],
-    )(core, hard, damping, damping_other, mine, theirs, first, own, other)
+        (pl.BlockSpec(memory_space=pl.ANY), VMEM),
+        [square] * 9 + [pltpu.VMEM((row_count, width), F32)] * 2 + [pltpu.SemaphoreType.DMA((2,))],
+    )(core, hard, damps, mine, theirs, first, own, other)
     return solved[None], score.reshape(row_count)
 
 

time: 257 us -> 256 us (level)
  transfers between devices with their start and end apart: 6 -> 6, of which waited for: 1 -> 2; matrix products, arithmetic and copies ran while one was open for 0% -> 0% of each run, Pallas kernels for 25% -> 25%
where the time goes in v7:
time: 256 us
  Pallas kernels  190 us (74%)
  blocking collectives  47.9 us (19%)
  starting transfers between devices  9.88 us (4%)
  waiting for transfers between devices  4.69 us (2%)
    pallas_call x1, Pallas kernels, on_device(): call(functools.partial(solve_kernel, count), (jax.ShapeDtypeStruct((row_c...  126 us
    pallas_call x1, Pallas kernels, on_device(): call(functools.partial(first_kernel, count), (matrix, jax.ShapeDtypeStruc...  62.5 us
    all_to_all x2, blocking collectives, exchanged(): lax.all_to_all(array.reshape(devices, 1, -1), axis, 0, 0, tiled=True)  47.9 us
    ppermute x3, starting transfers between devices, from_others(): lax.ppermute(array, axis, [(i, (i + shift) % devices) for i in range(devi...  9.29 us
  transfers between devices with their start and end apart: 6, of which 2 were waited for; matrix products, arithmetic and copies ran while one was open for 0% of the time, Pallas kernels for 25%

profile of v7, /device:TPU:8, one launch (start us, length us, event | category | flops | bytes accessed | tf_op | source)
XLA Modules:
  0.0 255.8 jit_solution(7044569250577941501)
XLA Ops:
  0.6 0.1 collective-permute-start.1
  0.7 0.5 collective-permute-start
  1.9 0.6 collective-permute-done.damp_other_ref
  2.5 0.0 copy-start
  2.5 0.9 copy-done
  3.4 0.0 copy-start.1
  3.4 0.7 copy-done.1
  4.1 0.8 shard_map.50
  4.9 0.0 collective-permute-done.1.other_ref
  4.9 0.4 shard_map.51
  5.3 26.8 %all_to_all.10 = f32[32,1,9216]{2,1,0:T(1,128)S(1)} all-to-all(f32[32,1,9216]{2,1,0:T(1,128)S(1)} %bitcast.10), channel_id=1, replica_groups=mesh['layer'=2,'z_hi'=4,'z_lo'=2,'y'=4,'x'=4] {'z_lo','y','x'}, dimensions={0} | all-to-all | bytes 2359296 | tf_op jit(solution)/shard_map/all_to_all | solution.py:331
  32.2 0.1 shard_map.52.refs_0_
  32.3 5.5 %collective-permute-start.4 = (f32[72,128]{1,0:T(8,128)S(1)}, f32[72,128]{1,0:T(8,128)S(1)}, u32[]{:S(2)}, u32[]{:S(2)}) collective-permute-start(f32[72,128]{1,0:T(8,128)S(1)} %shard_map.52.refs_0_), channel_id=1, source_target_pairs={{0,96},{32,0},{64,32},{96,64},{1,97},{33,1},{65,33},{97,65},{2,98}... | collective-permute-start | bytes 110600 | tf_op jit(solution)/shard_map/ppermute | solution.py:338
  37.7 1.4 collective-permute-start.3
  39.2 2.4 collective-permute-start.2
  41.5 0.0 collective-permute-done.4.refs_3_
  41.5 4.1 %collective-permute-done.3.refs_2_ = f32[72,128]{1,0:T(8,128)S(1)} collective-permute-done((f32[72,128]{1,0:T(8,128)S(1)}, f32[72,128]{1,0:T(8,128)S(1)}, u32[]{:S(2)}, u32[]{:S(2)}) %collective-permute-start.3) | collective-permute-done | bytes 36896 | tf_op jit(solution)/shard_map/ppermute | solution.py:338
  45.6 0.0 collective-permute-done.2.refs_1_
  45.6 0.1 shard_map.53
  45.7 21.0 %all_to_all.11 = f32[32,1,9216]{2,1,0:T(1,128)S(1)} all-to-all(f32[32,1,9216]{2,1,0:T(1,128)S(1)} %bitcast.9), channel_id=1, replica_groups=mesh['layer'=2,'z_hi'=4,'z_lo'=2,'y'=4,'x'=4] {'z_lo','y','x'}, dimensions={0} | all-to-all | bytes 2359296 | tf_op jit(solution)/shard_map/all_to_all | solution.py:331
  66.8 0.0 collective-permute-start.5
  66.8 62.5 %shard_map.54 = (f32[512,512]{1,0:T(8,128)S(1)}, s32[1]{0:T(128)}) custom-call(f32[16,128]{1,0:T(8,128)S(1)} %get-tuple-element.10.damp_ref.damps_ref, f32[2304,128]{1,0:T(8,128)S(1)} %bitcast.13), custom_call_target="tpu_custom_call" | custom-call | flops 3000000000 | bytes 1048576 | tf_op jit(solution)/shard_map/pallas_call | solution.py:383
  129.3 0.0 collective-permute-done.5.theirs_ref
  129.3 126.3 %shard_map.55 = (f32[256,512]{1,0:T(8,128)}, f32[1,256]{1,0:T(1,128)}) custom-call(s32[1]{0:T(128)} %bitcast.core_ref, s32[1]{0:T(128)} %get-tuple-element.14.hard_ref, f32[16,128]{1,0:T(8,128)S(1)} %get-tuple-element.10.damp_ref.damps_ref, f32[2304,128]{1,0:T(8,128)S(1)} %bitcast.14, f32[2304,128]{1,0:T(8,128)S(1)} %collective-permute-done.5.theirs_ref, ...), custom_call_target="tpu_custom_call" | custom-call | flops 6000000000 | bytes 1048576 | tf_op jit(solution)/shard_map/pallas_call | solution.py:392
Async XLA Ops:
  0.6 4.3 %collective-permute-start.1 = (bf16[256,512]{1,0:T(8,128)(2,1)}, bf16[256,512]{1,0:T(8,128)(2,1)S(1)}, u32[]{:S(2)}, u32[]{:S(2)}) collective-permute-start(bf16[256,512]{1,0:T(8,128)(2,1)} %bitcast.15), channel_id=1, source_target_pairs={{0,128},{128,0},{1,129},{129,1},{2,130},{130,2},{3,131},{131,3},{4... | collective-permute-start | bytes 786440 | tf_op jit(solution)/shard_map/ppermute | solution.py:350
  0.7 1.7 collective-permute-start
  2.5 1.0 copy-start
  3.4 0.7 copy-start.1
  32.3 9.3 %collective-permute-start.4 = (f32[72,128]{1,0:T(8,128)S(1)}, f32[72,128]{1,0:T(8,128)S(1)}, u32[]{:S(2)}, u32[]{:S(2)}) collective-permute-start(f32[72,128]{1,0:T(8,128)S(1)} %shard_map.52.refs_0_), channel_id=1, source_target_pairs={{0,96},{32,0},{64,32},{96,64},{1,97},{33,1},{65,33},{97,65},{2,98}... | collective-permute-start | bytes 110600 | tf_op jit(solution)/shard_map/ppermute | solution.py:338
  37.7 7.9 %collective-permute-start.3 = (f32[72,128]{1,0:T(8,128)S(1)}, f32[72,128]{1,0:T(8,128)S(1)}, u32[]{:S(2)}, u32[]{:S(2)}) collective-permute-start(f32[72,128]{1,0:T(8,128)S(1)} %shard_map.52.refs_0_), channel_id=1, source_target_pairs={{0,64},{32,96},{64,0},{96,32},{1,65},{33,97},{65,1},{97,33},{2,66}... | collective-permute-start | bytes 110600 | tf_op jit(solution)/shard_map/ppermute | solution.py:338
  39.2 6.5 %collective-permute-start.2 = (f32[72,128]{1,0:T(8,128)S(1)}, f32[72,128]{1,0:T(8,128)S(1)}, u32[]{:S(2)}, u32[]{:S(2)}) collective-permute-start(f32[72,128]{1,0:T(8,128)S(1)} %shard_map.52.refs_0_), channel_id=1, source_target_pairs={{0,32},{32,64},{64,96},{96,0},{1,33},{33,65},{65,97},{97,1},{2,34}... | collective-permute-start | bytes 110600 | tf_op jit(solution)/shard_map/ppermute | solution.py:338
  66.8 62.5 %collective-permute-start.5 = (f32[2304,128]{1,0:T(8,128)S(1)}, f32[2304,128]{1,0:T(8,128)S(1)}, u32[]{:S(2)}, u32[]{:S(2)}) collective-permute-start(f32[2304,128]{1,0:T(8,128)S(1)} %bitcast.12), channel_id=1, source_target_pairs={{0,128},{128,0},{1,129},{129,1},{2,130},{130,2},{3,131},{131,3},{4... | collective-permute-start | bytes 3538952 | tf_op jit(solution)/shard_map/ppermute | solution.py:382

commit v8 on v7

--- a/solution.py
+++ b/solution.py
@@ -49,25 +49,18 @@
     lax.fori_loop(0, TILES, step, 0)
 
 
-def mask_kernel(
-    damp_ref, damp_other_ref, labeled_hbm, own_hbm, own_t_ref, own_ref, keep_ref, damps_ref, labeled_ref, sems
+def mask_kernel(labeled_ref, own_ref, own_t_ref, rows_ref, keep_ref):
+    keep = (labeled_ref[...] > 0).astype(F32)
+    own_t_ref[...] = (own_ref[...].astype(F32).T * keep).astype(BF16)
+    rows_ref[...] = own_ref[...]
+    keep_ref[...] = keep
+
+
+def gram_kernel(
+    core_ref, damp_ref, damp_other_ref, keep_ref, own_t_ref, own_ref, other_ref, out_ref, damps_ref
 ):
-    arriving = [
-        pltpu.make_async_copy(own_hbm, own_ref, sems.at[0]),
-        pltpu.make_async_copy(labeled_hbm, labeled_ref, sems.at[1]),
-    ]
-    for copy in arriving:
-        copy.start()
     damps_ref[:8] = jnp.full((8, LANES), damp_ref[0])
     damps_ref[8:] = jnp.full((8, LANES), damp_other_ref[0])
-    for copy in arriving:
-        copy.wait()
-    keep = (labeled_ref[...] > 0).astype(F32)
-    own_t_ref[...] = (own_ref[...].astype(F32).T * keep).astype(BF16)
-    keep_ref[...] = keep
-
-
-def gram_kernel(core_ref, keep_ref, own_t_ref, own_ref, other_ref, out_ref):
     core = core_ref[0]
     keep = keep_ref[...]
     own_t, own, other = own_t_ref[...], own_ref[...], other_ref[...]
@@ -204,7 +197,7 @@
 def solve_kernel(
     count, core_ref, hard_ref, damps_ref, mine_ref, theirs_ref, first_ref, own_ref, other_ref,
     solved_ref, score_ref, s_ref, d_ref, c_ref, ct_ref, a_ref, x_ref, r_ref, t_ref, y_ref,
-    left_ref, z_ref, sems,
+    left_ref, z_ref, sem,
 ):
     near = core_ref[0] == 0
     width = own_ref.shape[1]
@@ -238,11 +231,7 @@
 
     hard = invert(s_ref, a_ref, x_ref, r_ref, t_ref, refresh, hard_ref[0] > 0)
 
-    half = z_ref.shape[0] // 2
-    parts = [pl.ds(0, half), pl.ds(half, half)]
-    leaving = [
-        pltpu.make_async_copy(z_ref.at[p], solved_ref.at[p], sems.at[i]) for i, p in enumerate(parts)
-    ]
+    leaving = pltpu.make_async_copy(z_ref, solved_ref, sem)
 
     def candidate_sum(terms):
         folded = terms[:, :LANES]
@@ -250,22 +239,15 @@
             folded = folded + terms[:, b * LANES : (b + 1) * LANES]
         return jnp.sum(folded.T, axis=0, keepdims=True)
 
-    def scores(p, z_own, z_other):
-        gain = own_ref[p, :].astype(F32) * z_own + other_ref[p, :].astype(F32) * z_other
-        gain = candidate_sum(gain)
-        penalty = damp * candidate_sum(z_own * z_own) + damp_other * candidate_sum(z_other * z_other)
-        return (gain - penalty) / (1.0 + gain)
-
-    def outputs(solve_rows):
-        found = []
-        for p, copy in zip(parts, leaving):
-            z_own, z_other = solve_rows(p)
-            z_ref[p, :] = z_own
-            copy.start()
-            found.append((p, z_own, z_other))
-        score_ref[...] = jnp.concatenate([scores(*each) for each in found], axis=1)
-        for copy in leaving:
-            copy.wait()
+    def outputs(z_own, z_other):
+        z_ref[...] = z_own
+        leaving.start()
+        gain = candidate_sum(own_ref[...].astype(F32) * z_own + other_ref[...].astype(F32) * z_other)
+        wide = (z_own.shape[0] // LANES,)
+        penalty = jnp.tile(damp, wide) * candidate_sum(z_own * z_own)
+        penalty = penalty + jnp.tile(damp_other, wide) * candidate_sum(z_other * z_other)
+        score_ref[...] = (gain - penalty) / (1.0 + gain)
+        leaving.wait()
 
     @pl.when(hard)
     def _():
@@ -292,24 +274,19 @@
             return carry
 
         lax.fori_loop(0, REFINEMENTS, refine, 0)
-        outputs(lambda p: (z_own[p, :], z_other[p, :]))
+        outputs(z_own[...], z_other[...])
 
     @pl.when(jnp.logical_not(hard))
     def _():
-        y, x, p0 = split(y_ref[...]), split(x_ref[...]), split(first_ref[...])
-
-        def solve_rows(p):
-            own = (own_ref[p, :],)
-            left = other_ref[p, :].astype(F32) - dot_split(own, y)
-            z_other = dot_split(split(left), x)
-            return dot_split(own, p0) - dot_split(split(z_other), y, ((1,), (1,))), z_other
-
-        outputs(solve_rows)
+        own, y = (own_ref[...],), split(y_ref[...])
+        left = other_ref[...].astype(F32) - dot_split(own, y)
+        z_other = dot_split(split(left), split(x_ref[...]))
+        z_own = dot_split(own, split(first_ref[...])) - dot_split(split(z_other), y, ((1,), (1,)))
+        outputs(z_own, z_other)
 
 
 SMEM = pl.BlockSpec(memory_space=pltpu.SMEM)
 VMEM = pl.BlockSpec(memory_space=pltpu.VMEM)
-HBM = pl.BlockSpec(memory_space=pltpu.HBM)
 
 
 def call(kernel, out_shape, in_specs, mebibytes, megaflops=0, out_specs=VMEM, scratch=()):
@@ -358,23 +335,26 @@
     def slabs(length):
         return jax.ShapeDtypeStruct((length, LANES), F32)
 
-    own_t, own, keep, damps = call(
+    own_t, own, keep = call(
         mask_kernel,
         (
             jax.ShapeDtypeStruct((width, row_count), BF16),
             jax.ShapeDtypeStruct((row_count, width), BF16),
             jax.ShapeDtypeStruct((1, row_count), F32),
-            jax.ShapeDtypeStruct((16, LANES), F32),
         ),
-        [SMEM, SMEM, HBM, HBM],
+        [VMEM] * 2,
         8,
         2000,
-        (VMEM,) * 4,
-        [pltpu.VMEM((1, row_count), jnp.int32), pltpu.SemaphoreType.DMA((2,))],
-    )(damping, damping_other, labeled, own)
-    products = call(gram_kernel, slabs(rows), [SMEM] + [VMEM] * 4, 16, 500)(
-        core, keep, own_t, own, other
-    )
+        (VMEM,) * 3,
+    )(labeled, own)
+    products, damps = call(
+        gram_kernel,
+        (slabs(rows), slabs(16)),
+        [SMEM] * 3 + [VMEM] * 4,
+        16,
+        500,
+        (VMEM,) * 2,
+    )(core, damping, damping_other, keep, own_t, own, other)
     partial = call(sum_kernel, slabs(rows // pieces), [VMEM], 8, 50)(exchanged(products, NEAR))
     partials = [partial, *from_others(partial, FAR)]
     total = call(total_kernel, slabs(rows), [VMEM] * planes, 8, 50)(*partials)
@@ -399,7 +379,7 @@
         32,
         6000,
         (pl.BlockSpec(memory_space=pl.ANY), VMEM),
-        [square] * 9 + [pltpu.VMEM((row_count, width), F32)] * 2 + [pltpu.SemaphoreType.DMA((2,))],
+        [square] * 9 + [pltpu.VMEM((row_count, width), F32)] * 2 + [pltpu.SemaphoreType.DMA],
     )(core, hard, damps, mine, theirs, first, own, other)
     return solved[None], score.reshape(row_count)
 

time: 256 us -> 257 us (level)
  transfers between devices with their start and end apart: 6 -> 6, of which waited for: 2 -> 1; matrix products, arithmetic and copies ran while one was open for 0% -> 0% of each run, Pallas kernels for 25% -> 25%
where the time goes in v8:
time: 257 us; the launch traced here: 255 us
  Pallas kernels  190 us (74%)
  blocking collectives  47.9 us (19%)
  starting transfers between devices  9.88 us (4%)
  waiting for transfers between devices  4.1 us (2%)
    pallas_call x1, Pallas kernels, on_device(): call(functools.partial(solve_kernel, count), (jax.ShapeDtypeStruct((row_c...  127 us
    pallas_call x1, Pallas kernels, on_device(): call(functools.partial(first_kernel, count), (matrix, jax.ShapeDtypeStruc...  62.5 us
    all_to_all x2, blocking collectives, exchanged(): lax.all_to_all(array.reshape(devices, 1, -1), axis, 0, 0, tiled=True)  47.9 us
    ppermute x3, starting transfers between devices, from_others(): lax.ppermute(array, axis, [(i, (i + shift) % devices) for i in range(devi...  9.29 us
  transfers between devices with their start and end apart: 6, of which 1 were waited for; matrix products, arithmetic and copies ran while one was open for 0% of the time, Pallas kernels for 25%

profile of v8, /device:TPU:8, one launch (start us, length us, event | category | flops | bytes accessed | tf_op | source)
XLA Modules:
  0.0 255.4 jit_solution(8153107622169239709)
XLA Ops:
  0.6 0.1 collective-permute-start.1
  0.7 0.5 collective-permute-start
  1.9 0.0 copy-start
  1.9 0.9 copy-done
  2.8 0.0 copy-start.1
  2.8 0.7 copy-done.1
  3.5 0.1 shard_map.50
  3.7 0.0 collective-permute-done.damp_other_ref
  3.7 0.0 collective-permute-done.1.other_ref
  3.7 1.0 shard_map.51
  4.7 26.8 %all_to_all.10 = f32[32,1,9216]{2,1,0:T(1,128)S(1)} all-to-all(f32[32,1,9216]{2,1,0:T(1,128)S(1)} %bitcast.14), channel_id=1, replica_groups=mesh['layer'=2,'z_hi'=4,'z_lo'=2,'y'=4,'x'=4] {'z_lo','y','x'}, dimensions={0} | all-to-all | bytes 2359296 | tf_op jit(solution)/shard_map/all_to_all | solution.py:308
  31.5 0.1 shard_map.52.refs_0_
  31.6 5.5 %collective-permute-start.4 = (f32[72,128]{1,0:T(8,128)S(1)}, f32[72,128]{1,0:T(8,128)S(1)}, u32[]{:S(2)}, u32[]{:S(2)}) collective-permute-start(f32[72,128]{1,0:T(8,128)S(1)} %shard_map.52.refs_0_), channel_id=1, source_target_pairs={{0,96},{32,0},{64,32},{96,64},{1,97},{33,1},{65,33},{97,65},{2,98}... | collective-permute-start | bytes 110600 | tf_op jit(solution)/shard_map/ppermute | solution.py:315
  37.1 1.4 collective-permute-start.3
  38.5 2.4 collective-permute-start.2
  40.9 0.0 collective-permute-done.4.refs_3_
  40.9 4.1 %collective-permute-done.3.refs_2_ = f32[72,128]{1,0:T(8,128)S(1)} collective-permute-done((f32[72,128]{1,0:T(8,128)S(1)}, f32[72,128]{1,0:T(8,128)S(1)}, u32[]{:S(2)}, u32[]{:S(2)}) %collective-permute-start.3) | collective-permute-done | bytes 36896 | tf_op jit(solution)/shard_map/ppermute | solution.py:315
  45.0 0.0 collective-permute-done.2.refs_1_
  45.0 0.1 shard_map.53
  45.1 21.1 %all_to_all.11 = f32[32,1,9216]{2,1,0:T(1,128)S(1)} all-to-all(f32[32,1,9216]{2,1,0:T(1,128)S(1)} %bitcast.9), channel_id=1, replica_groups=mesh['layer'=2,'z_hi'=4,'z_lo'=2,'y'=4,'x'=4] {'z_lo','y','x'}, dimensions={0} | all-to-all | bytes 2359296 | tf_op jit(solution)/shard_map/all_to_all | solution.py:308
  66.1 0.0 collective-permute-start.5
  66.1 62.5 %shard_map.54 = (f32[512,512]{1,0:T(8,128)S(1)}, s32[1]{0:T(128)}) custom-call(f32[16,128]{1,0:T(8,128)S(1)} %get-tuple-element.14.damp_ref.damps_ref, f32[2304,128]{1,0:T(8,128)S(1)} %bitcast.12), custom_call_target="tpu_custom_call" | custom-call | flops 3000000000 | bytes 1048576 | tf_op jit(solution)/shard_map/pallas_call | solution.py:363
  128.7 0.0 collective-permute-done.5.theirs_ref
  128.7 126.5 %shard_map.55 = (f32[256,512]{1,0:T(8,128)}, f32[1,256]{1,0:T(1,128)}) custom-call(s32[1]{0:T(128)} %bitcast.core_ref, s32[1]{0:T(128)} %get-tuple-element.16.hard_ref, f32[16,128]{1,0:T(8,128)S(1)} %get-tuple-element.14.damp_ref.damps_ref, f32[2304,128]{1,0:T(8,128)S(1)} %bitcast.13, f32[2304,128]{1,0:T(8,128)S(1)} %collective-permute-done.5.theirs_ref, ...), custom_call_target="tpu_custom_call" | custom-call | flops 6000000000 | bytes 1048576 | tf_op jit(solution)/shard_map/pallas_call | solution.py:372
Async XLA Ops:
  0.6 3.0 %collective-permute-start.1 = (bf16[256,512]{1,0:T(8,128)(2,1)}, bf16[256,512]{1,0:T(8,128)(2,1)S(1)}, u32[]{:S(2)}, u32[]{:S(2)}) collective-permute-start(bf16[256,512]{1,0:T(8,128)(2,1)} %bitcast.15), channel_id=1, source_target_pairs={{0,128},{128,0},{1,129},{129,1},{2,130},{130,2},{3,131},{131,3},{4... | collective-permute-start | bytes 786440 | tf_op jit(solution)/shard_map/ppermute | solution.py:327
  0.7 2.9 %collective-permute-start = (f32[1]{0:T(128)}, f32[1]{0:T(128)}, u32[]{:S(2)}, u32[]{:S(2)}) collective-permute-start(f32[1]{0:T(128)} %param.5), channel_id=1, source_target_pairs={{0,128},{128,0},{1,129},{129,1},{2,130},{130,2},{3,131},{131,3},{4... | collective-permute-start | bytes 20 | tf_op jit(solution)/shard_map/ppermute | solution.py:328
  1.9 1.0 copy-start
  2.8 0.7 copy-start.1
  31.6 9.3 %collective-permute-start.4 = (f32[72,128]{1,0:T(8,128)S(1)}, f32[72,128]{1,0:T(8,128)S(1)}, u32[]{:S(2)}, u32[]{:S(2)}) collective-permute-start(f32[72,128]{1,0:T(8,128)S(1)} %shard_map.52.refs_0_), channel_id=1, source_target_pairs={{0,96},{32,0},{64,32},{96,64},{1,97},{33,1},{65,33},{97,65},{2,98}... | collective-permute-start | bytes 110600 | tf_op jit(solution)/shard_map/ppermute | solution.py:315
  37.1 7.9 %collective-permute-start.3 = (f32[72,128]{1,0:T(8,128)S(1)}, f32[72,128]{1,0:T(8,128)S(1)}, u32[]{:S(2)}, u32[]{:S(2)}) collective-permute-start(f32[72,128]{1,0:T(8,128)S(1)} %shard_map.52.refs_0_), channel_id=1, source_target_pairs={{0,64},{32,96},{64,0},{96,32},{1,65},{33,97},{65,1},{97,33},{2,66}... | collective-permute-start | bytes 110600 | tf_op jit(solution)/shard_map/ppermute | solution.py:315
  38.5 6.5 %collective-permute-start.2 = (f32[72,128]{1,0:T(8,128)S(1)}, f32[72,128]{1,0:T(8,128)S(1)}, u32[]{:S(2)}, u32[]{:S(2)}) collective-permute-start(f32[72,128]{1,0:T(8,128)S(1)} %shard_map.52.refs_0_), channel_id=1, source_target_pairs={{0,32},{32,64},{64,96},{96,0},{1,33},{33,65},{65,97},{97,1},{2,34}... | collective-permute-start | bytes 110600 | tf_op jit(solution)/shard_map/ppermute | solution.py:315
  66.1 62.5 %collective-permute-start.5 = (f32[2304,128]{1,0:T(8,128)S(1)}, f32[2304,128]{1,0:T(8,128)S(1)}, u32[]{:S(2)}, u32[]{:S(2)}) collective-permute-start(f32[2304,128]{1,0:T(8,128)S(1)} %bitcast.11), channel_id=1, source_target_pairs={{0,128},{128,0},{1,129},{129,1},{2,130},{130,2},{3,131},{131,3},{4... | collective-permute-start | bytes 3538952 | tf_op jit(solution)/shard_map/ppermute | solution.py:362

commit v9 on v8

--- a/solution.py
+++ b/solution.py
@@ -13,10 +13,15 @@
 F32, BF16 = jnp.float32, jnp.bfloat16
 LANES = 128
 HALF = LANES // 2
+DIAGONAL = HALF + HALF // 2
 RESIDUAL = 0.002
 STEPS = 60
 TILES = 4
 REFINEMENTS = 3
+
+
+def slab_rows(blocks):
+    return DIAGONAL + (blocks - 1) * LANES + HALF
 
 
 def dot(a, b, dims=((1,), (0,)), precision=None):
@@ -49,18 +54,21 @@
     lax.fori_loop(0, TILES, step, 0)
 
 
-def mask_kernel(labeled_ref, own_ref, own_t_ref, rows_ref, keep_ref):
+def mask_kernel(labeled_hbm, own_hbm, own_t_ref, own_ref, keep_ref, labeled_ref, sems):
+    arriving = [
+        pltpu.make_async_copy(own_hbm, own_ref, sems.at[0]),
+        pltpu.make_async_copy(labeled_hbm, labeled_ref, sems.at[1]),
+    ]
+    for copy in arriving:
+        copy.start()
+    for copy in arriving:
+        copy.wait()
     keep = (labeled_ref[...] > 0).astype(F32)
     own_t_ref[...] = (own_ref[...].astype(F32).T * keep).astype(BF16)
-    rows_ref[...] = own_ref[...]
     keep_ref[...] = keep
 
 
-def gram_kernel(
-    core_ref, damp_ref, damp_other_ref, keep_ref, own_t_ref, own_ref, other_ref, out_ref, damps_ref
-):
-    damps_ref[:8] = jnp.full((8, LANES), damp_ref[0])
-    damps_ref[8:] = jnp.full((8, LANES), damp_other_ref[0])
+def gram_kernel(core_ref, keep_ref, own_t_ref, own_ref, other_ref, out_ref):
     core = core_ref[0]
     keep = keep_ref[...]
     own_t, own, other = own_t_ref[...], own_ref[...], other_ref[...]
@@ -68,16 +76,27 @@
     first_t = jnp.where(core == 0, own_t, (other.astype(F32).T * keep).astype(BF16))
     last = jnp.where(core == 0, other, own)
     both = jnp.concatenate([own, other], axis=1)
-    slab = blocks * LANES + HALF
+    slab = slab_rows(blocks)
+    left = lax.broadcasted_iota(jnp.int32, (HALF // 2, LANES), 1) < HALF
     for i in range(blocks):
         rows = own_t[i * LANES : (i + 1) * LANES]
         product = dot(rows, both[:, i * LANES : (i + blocks) * LANES])
-        for b in range(blocks):
-            start = i * slab + b * LANES
+        start = i * slab
+        out_ref[start : start + HALF] = product[:HALF, :LANES]
+        upper, lower = product[HALF : HALF + HALF // 2, :LANES], product[HALF + HALF // 2 :, :LANES]
+        start = i * slab + HALF
+        out_ref[start : start + HALF // 2] = jnp.where(left, pltpu.roll(upper, HALF, 1), lower)
+        for b in range(1, blocks):
+            start = i * slab + DIAGONAL + (b - 1) * LANES
             out_ref[start : start + LANES] = product[:, b * LANES : (b + 1) * LANES]
         middle = dot(first_t[i * LANES : (i + 1) * LANES], last[:, i * LANES : (i + 1) * LANES])
-        start = i * slab + blocks * LANES
+        start = (i + 1) * slab - HALF
         out_ref[start : start + HALF] = jnp.where(core == 0, middle[:HALF], middle[HALF:])
+
+
+def damp_kernel(damp_ref, damp_other_ref, damps_ref):
+    damps_ref[:8] = jnp.full((8, LANES), damp_ref[0])
+    damps_ref[8:] = jnp.full((8, LANES), damp_other_ref[0])
 
 
 def sum_kernel(in_ref, out_ref):
@@ -170,8 +189,21 @@
 
 
 def part(ref, i, start, rows, blocks, count):
-    at = i * (blocks * LANES + HALF) + start
+    at = i * slab_rows(blocks) + start
     return ref[at : at + rows] * (1.0 / count)
+
+
+def whole_part(ref, i, b, blocks, count):
+    return part(ref, i, DIAGONAL + (b - 1) * LANES, LANES, blocks, count)
+
+
+def diagonal_part(ref, i, blocks, count):
+    upper = part(ref, i, 0, HALF, blocks, count)
+    packed = part(ref, i, HALF, HALF // 2, blocks, count)
+    corner = jnp.concatenate([pltpu.roll(packed, HALF, 1), packed], axis=0)
+    left = lax.broadcasted_iota(jnp.int32, (HALF, LANES), 1) < HALF
+    turned = jnp.concatenate([upper, corner], axis=0).T
+    return jnp.concatenate([upper, jnp.where(left, turned[HALF:], corner)], axis=0)
 
 
 def put(ref, i, j, block):
@@ -182,9 +214,9 @@
     blocks = ref.shape[0] // LANES
     unit = eye(LANES)
     for i in range(blocks):
-        put(ref, i, i, part(slabs_ref, i, 0, LANES, blocks, count) + jnp.where(unit, damp, 0.0))
+        put(ref, i, i, diagonal_part(slabs_ref, i, blocks, count) + jnp.where(unit, damp, 0.0))
         for j in range(i + 1, blocks):
-            block = part(slabs_ref, i, (j - i) * LANES, LANES, blocks, count)
+            block = whole_part(slabs_ref, i, j - i, blocks, count)
             put(ref, i, j, block)
             put(ref, j, i, block.T)
 
@@ -206,15 +238,15 @@
 
     for i in range(blocks):
         for j in range(i):
-            start = (j + blocks - i) * LANES
-            block = part(mine_ref, i, start, LANES, blocks, count)
+            block = whole_part(mine_ref, i, j + blocks - i, blocks, count)
             put(c_ref, i, j, block)
             put(ct_ref, j, i, block.T)
-            block = part(theirs_ref, i, start, LANES, blocks, count)
+            block = whole_part(theirs_ref, i, j + blocks - i, blocks, count)
             put(ct_ref, i, j, block)
             put(c_ref, j, i, block.T)
-        mine = part(mine_ref, i, blocks * LANES, HALF, blocks, count)
-        theirs = part(theirs_ref, i, blocks * LANES, HALF, blocks, count)
+        last = slab_rows(blocks) - HALF
+        mine = part(mine_ref, i, last, HALF, blocks, count)
+        theirs = part(theirs_ref, i, last, HALF, blocks, count)
         block = jnp.concatenate([jnp.where(near, mine, theirs), jnp.where(near, theirs, mine)], 0)
         turned = block.T
         put(c_ref, i, i, jnp.where(near, block, turned))
@@ -325,10 +357,9 @@
     own = grads[0]
     labeled = labeled.reshape(1, row_count)
     other = lax.ppermute(own, "layer", swap)
-    damping_other = lax.ppermute(damping, "layer", swap)
     blocks = width // LANES
-    rows = blocks * (blocks * LANES + HALF)
-    pieces, planes = lax.axis_size(NEAR), lax.axis_size(FAR)
+    rows = blocks * slab_rows(blocks)
+    planes = lax.axis_size(FAR)
     square = pltpu.VMEM((width, width), F32)
     matrix = jax.ShapeDtypeStruct((width, width), F32)
 
@@ -342,21 +373,25 @@
             jax.ShapeDtypeStruct((row_count, width), BF16),
             jax.ShapeDtypeStruct((1, row_count), F32),
         ),
-        [VMEM] * 2,
+        [pl.BlockSpec(memory_space=pltpu.HBM)] * 2,
         8,
         2000,
         (VMEM,) * 3,
-    )(labeled, own)
-    products, damps = call(
-        gram_kernel,
-        (slabs(rows), slabs(16)),
-        [SMEM] * 3 + [VMEM] * 4,
-        16,
-        500,
-        (VMEM,) * 2,
-    )(core, damping, damping_other, keep, own_t, own, other)
-    partial = call(sum_kernel, slabs(rows // pieces), [VMEM], 8, 50)(exchanged(products, NEAR))
+        [pltpu.VMEM((1, row_count), jnp.int32), pltpu.SemaphoreType.DMA((2,))],
+    )(
+        pltpu.with_memory_space_constraint(labeled, pltpu.HBM),
+        pltpu.with_memory_space_constraint(own, pltpu.HBM),
+    )
+    products = call(gram_kernel, slabs(rows), [SMEM] + [VMEM] * 4, 16, 500)(
+        core, keep, own_t, own, other
+    )
+    sheet = exchanged(products, NEAR)
+    partial = call(sum_kernel, slabs(rows // lax.axis_size(NEAR)), [VMEM], 8, 50)(sheet)
+    partial, damping = lax.optimization_barrier((partial, damping))
     partials = [partial, *from_others(partial, FAR)]
+    damping_other = lax.ppermute(damping, "layer", swap)
+    damps = call(damp_kernel, slabs(16), [SMEM] * 2, 8, 50)(damping, damping_other)
+    *partials, damps = lax.optimization_barrier((*partials, damps))
     total = call(total_kernel, slabs(rows), [VMEM] * planes, 8, 50)(*partials)
     mine = exchanged(total, NEAR)
     theirs = lax.ppermute(mine, "layer", swap)

time: 257 us -> 253 us (0.984)
    ppermute x3, waiting for transfers between devices: 4.09 us -> 1.48 us  [from_others(): lax.ppermute(array, axis, [(i, (i + shift) % devices) for i in range(devi...]
  transfers between devices with their start and end apart: 6 -> 6, of which waited for: 1 -> 4; matrix products, arithmetic and copies ran while one was open for 0% -> 0% of each run, Pallas kernels for 25% -> 25%
where the time goes in v9:
time: 253 us
  Pallas kernels  191 us (75%)
  blocking collectives  47.2 us (19%)
  starting transfers between devices  9.49 us (4%)
  waiting for transfers between devices  3.35 us (1%)
    pallas_call x1, Pallas kernels, on_device(): call(functools.partial(solve_kernel, count), (jax.ShapeDtypeStruct((row_c...  126 us
    pallas_call x1, Pallas kernels, on_device(): call(functools.partial(first_kernel, count), (matrix, jax.ShapeDtypeStruc...  62.7 us
    all_to_all x2, blocking collectives, exchanged(): lax.all_to_all(array.reshape(devices, 1, -1), axis, 0, 0, tiled=True)  47.2 us
    ppermute x3, starting transfers between devices, from_others(): lax.ppermute(array, axis, [(i, (i + shift) % devices) for i in range(devi...  9.29 us
  transfers between devices with their start and end apart: 6, of which 4 were waited for; matrix products, arithmetic and copies ran while one was open for 0% of the time, Pallas kernels for 25%

profile of v9, /device:TPU:8, one launch (start us, length us, event | category | flops | bytes accessed | tf_op | source)
XLA Modules:
  0.0 253.0 jit_solution(16032529716426053085)
XLA Ops:
  0.6 0.1 collective-permute-start
  0.7 1.1 shard_map.50
  1.9 0.6 collective-permute-done.other_ref
  2.5 0.4 shard_map.51
  2.9 26.3 %all_to_all.10 = f32[32,1,8704]{2,1,0:T(1,128)S(1)} all-to-all(f32[32,1,8704]{2,1,0:T(1,128)S(1)} %bitcast.10), channel_id=1, replica_groups=mesh['layer'=2,'z_hi'=4,'z_lo'=2,'y'=4,'x'=4] {'z_lo','y','x'}, dimensions={0} | all-to-all | bytes 2228224 | tf_op jit(solution)/shard_map/all_to_all | solution.py:340
  29.2 0.1 shard_map.52.refs_0_
  29.2 5.5 %collective-permute-start.3 = (f32[68,128]{1,0:T(8,128)S(1)}, f32[68,128]{1,0:T(8,128)S(1)}, u32[]{:S(2)}, u32[]{:S(2)}) collective-permute-start(f32[68,128]{1,0:T(8,128)S(1)} %shard_map.52.refs_0_), channel_id=1, source_target_pairs={{0,96},{32,0},{64,32},{96,64},{1,97},{33,1},{65,33},{97,65},{2,98}... | collective-permute-start | bytes 104456 | tf_op jit(solution)/shard_map/ppermute | solution.py:347
  34.7 1.4 collective-permute-start.2
  36.2 2.4 collective-permute-start.1
  39.2 0.1 collective-permute-start.4
  39.3 1.3 collective-permute-done.4.damp_other_ref
  40.6 0.6 shard_map.53.damp_ref.damps_ref
  41.2 0.0 collective-permute-done.3.refs_3_
  41.2 1.4 collective-permute-done.2.refs_2_
  42.6 0.1 collective-permute-done.1.refs_1_
  42.7 0.1 shard_map.54
  42.8 21.0 %all_to_all.11 = f32[32,1,8704]{2,1,0:T(1,128)S(1)} all-to-all(f32[32,1,8704]{2,1,0:T(1,128)S(1)} %bitcast.9), channel_id=1, replica_groups=mesh['layer'=2,'z_hi'=4,'z_lo'=2,'y'=4,'x'=4] {'z_lo','y','x'}, dimensions={0} | all-to-all | bytes 2228224 | tf_op jit(solution)/shard_map/all_to_all | solution.py:340
  63.7 0.0 collective-permute-start.5
  63.7 62.7 %shard_map.55 = (f32[512,512]{1,0:T(8,128)S(1)}, s32[1]{0:T(128)}) custom-call(f32[16,128]{1,0:T(8,128)S(1)} %shard_map.53.damp_ref.damps_ref, f32[2176,128]{1,0:T(8,128)S(1)} %bitcast.13), custom_call_target="tpu_custom_call" | custom-call | flops 3000000000 | bytes 1048576 | tf_op jit(solution)/shard_map/pallas_call | solution.py:398
  126.4 0.0 collective-permute-done.5.theirs_ref
  126.4 126.4 %shard_map.56 = (f32[256,512]{1,0:T(8,128)}, f32[1,256]{1,0:T(1,128)}) custom-call(s32[1]{0:T(128)} %bitcast.core_ref, s32[1]{0:T(128)} %get-tuple-element.26.hard_ref, f32[16,128]{1,0:T(8,128)S(1)} %shard_map.53.damp_ref.damps_ref, f32[2176,128]{1,0:T(8,128)S(1)} %bitcast.14, f32[2176,128]{1,0:T(8,128)S(1)} %collective-permute-done.5.theirs_ref, ...), custom_call_target="tpu_custom_call" | custom-call | flops 6000000000 | bytes 1048576 | tf_op jit(solution)/shard_map/pallas_call | solution.py:407
Async XLA Ops:
  0.6 1.8 collective-permute-start
  29.2 11.9 %collective-permute-start.3 = (f32[68,128]{1,0:T(8,128)S(1)}, f32[68,128]{1,0:T(8,128)S(1)}, u32[]{:S(2)}, u32[]{:S(2)}) collective-permute-start(f32[68,128]{1,0:T(8,128)S(1)} %shard_map.52.refs_0_), channel_id=1, source_target_pairs={{0,96},{32,0},{64,32},{96,64},{1,97},{33,1},{65,33},{97,65},{2,98}... | collective-permute-start | bytes 104456 | tf_op jit(solution)/shard_map/ppermute | solution.py:347
  34.7 7.9 %collective-permute-start.2 = (f32[68,128]{1,0:T(8,128)S(1)}, f32[68,128]{1,0:T(8,128)S(1)}, u32[]{:S(2)}, u32[]{:S(2)}) collective-permute-start(f32[68,128]{1,0:T(8,128)S(1)} %shard_map.52.refs_0_), channel_id=1, source_target_pairs={{0,64},{32,96},{64,0},{96,32},{1,65},{33,97},{65,1},{97,33},{2,66}... | collective-permute-start | bytes 104456 | tf_op jit(solution)/shard_map/ppermute | solution.py:347
  36.2 6.5 %collective-permute-start.1 = (f32[68,128]{1,0:T(8,128)S(1)}, f32[68,128]{1,0:T(8,128)S(1)}, u32[]{:S(2)}, u32[]{:S(2)}) collective-permute-start(f32[68,128]{1,0:T(8,128)S(1)} %shard_map.52.refs_0_), channel_id=1, source_target_pairs={{0,32},{32,64},{64,96},{96,0},{1,33},{33,65},{65,97},{97,1},{2,34}... | collective-permute-start | bytes 104456 | tf_op jit(solution)/shard_map/ppermute | solution.py:347
  39.2 1.4 collective-permute-start.4
  63.7 62.7 %collective-permute-start.5 = (f32[2176,128]{1,0:T(8,128)S(1)}, f32[2176,128]{1,0:T(8,128)S(1)}, u32[]{:S(2)}, u32[]{:S(2)}) collective-permute-start(f32[2176,128]{1,0:T(8,128)S(1)} %bitcast.12), channel_id=1, source_target_pairs={{0,128},{128,0},{1,129},{129,1},{2,130},{130,2},{3,131},{131,3},{4... | collective-permute-start | bytes 3342344 | tf_op jit(solution)/shard_map/ppermute | solution.py:397

commit v10 on v9

--- a/solution.py
+++ b/solution.py
@@ -122,70 +122,61 @@
     return rows == lax.broadcasted_iota(jnp.int32, (width, width), 1)
 
 
-def invert(s_ref, a_ref, x_ref, r_ref, t_ref, refresh=None, known_hard=None):
-    width = s_ref.shape[0]
-
-    def scales():
-        diagonal = jnp.where(eye(width), s_ref[...], 0.0)
-        row = lax.rsqrt(jnp.sum(diagonal, axis=0, keepdims=True))
-        return lax.rsqrt(jnp.sum(diagonal, axis=1, keepdims=True)), row
-
-    def scaled():
-        column, row = scales()
-        a_ref[...] = s_ref[...] * column * row
-
-    def square():
-        r = r_ref[...].astype(BF16)
-        t = dot(r, r)
-        t_ref[...] = t
-        return jnp.sum(t * t)
-
-    def residual():
-        dot_full(r_ref, a_ref, x_ref)
-        r_ref[...] = eye(width).astype(F32) - r_ref[...]
-
-    scaled()
-    one = eye(width).astype(F32)
-    e = one - a_ref[...]
+def scales(s_ref):
+    diagonal = jnp.where(eye(s_ref.shape[0]), s_ref[...], 0.0)
+    row = lax.rsqrt(jnp.sum(diagonal, axis=0, keepdims=True))
+    return lax.rsqrt(jnp.sum(diagonal, axis=1, keepdims=True)), row
+
+
+def near_inverse(s_ref, x_ref):
+    column, row = scales(s_ref)
+    a = s_ref[...] * column * row
+    one = eye(s_ref.shape[0]).astype(F32)
+    e = one - a
     e1 = e.astype(BF16)
     e2 = dot(e1, e1).astype(BF16)
     x = one + e
     x = (x + dot(x.astype(BF16), e2)).astype(BF16)
-    x_ref[...] = x.astype(F32)
-    r_ref[...] = one - dot_split(split(a_ref[...]), (x,))
-    norm = square()
-    hard = jnp.logical_not(norm <= RESIDUAL**2)
-    if known_hard is not None:
-        hard = jnp.logical_or(hard, known_hard)
-
-    @pl.when(hard)
+    r = one - dot_split(split(a), (x,))
+    r1 = r.astype(BF16)
+    r2 = dot(r1, r1)
+    x_ref[...] = (x.astype(F32) + dot(x, (r + r2).astype(BF16))) * column * row
+    return jnp.logical_not(jnp.sum(r2 * r2) <= RESIDUAL**2)
+
+
+def full_inverse(s_ref, x_ref, a_ref, r_ref, t_ref):
+    width = s_ref.shape[0]
+
+    def residual():
+        dot_full(r_ref, a_ref, x_ref)
+        r_ref[...] = eye(width).astype(F32) - r_ref[...]
+        return jnp.sum(r_ref[...] * r_ref[...])
+
+    column, row = scales(s_ref)
+    a_ref[...] = s_ref[...] * column * row
+    x_ref[...] = x_ref[...] / (column * row)
+    norm = residual()
+    contracts = norm < 0.25
+
+    @pl.when(jnp.logical_not(contracts))
     def _():
-        if refresh is not None:
-            refresh()
-        scaled()
-
-        @pl.when(jnp.logical_not(norm < 0.25))
-        def _():
-            largest = jnp.max(jnp.sum(jnp.abs(a_ref[...]), axis=1, keepdims=True))
-            x_ref[...] = jnp.where(eye(width), 1.0 / largest, 0.0)
-
+        largest = jnp.max(jnp.sum(jnp.abs(a_ref[...]), axis=1, keepdims=True))
+        x_ref[...] = jnp.where(eye(width), 1.0 / largest, 0.0)
         residual()
 
-        def far(state):
-            return jnp.logical_and(state[0] < STEPS, state[1] > 0.01 * RESIDUAL**2)
-
-        def newton(state):
-            dot_full(t_ref, x_ref, r_ref)
-            x_ref[...] += t_ref[...]
-            residual()
-            return state[0] + 1, square()
-
-        lax.while_loop(far, newton, (jnp.int32(0), square()))
-
-    step = (r_ref[...] + t_ref[...]).astype(BF16)
-    column, row = scales()
-    x_ref[...] = (x_ref[...] + dot(x_ref[...].astype(BF16), step)) * column * row
-    return hard
+    def far(state):
+        return jnp.logical_and(state[0] < STEPS, jnp.logical_not(state[1] <= RESIDUAL**2))
+
+    def newton(state):
+        dot_full(t_ref, x_ref, r_ref)
+        x_ref[...] += t_ref[...]
+        return state[0] + 1, residual()
+
+    start = jnp.where(contracts, norm, jnp.float32(width))
+    lax.while_loop(far, newton, (jnp.int32(0), start))
+    dot_full(t_ref, x_ref, r_ref)
+    column, row = scales(s_ref)
+    x_ref[...] = (x_ref[...] + t_ref[...]) * column * row
 
 
 def part(ref, i, start, rows, blocks, count):
@@ -223,7 +214,12 @@
 
 def first_kernel(count, damp_ref, mine_ref, x_ref, hard_ref, s_ref, a_ref, r_ref, t_ref):
     put_diagonal(s_ref, mine_ref, damp_ref[:1], count)
-    hard_ref[0] = invert(s_ref, a_ref, x_ref, r_ref, t_ref).astype(jnp.int32)
+    hard = near_inverse(s_ref, x_ref)
+    hard_ref[0] = hard.astype(jnp.int32)
+
+    @pl.when(hard)
+    def _():
+        full_inverse(s_ref, x_ref, a_ref, r_ref, t_ref)
 
 
 def solve_kernel(
@@ -257,12 +253,7 @@
     y_ref[...] = dot_split(first, split(c_ref[...]))
     s_ref[...] = d_ref[...] - dot_split(split(ct_ref[...]), split(y_ref[...]))
 
-    def refresh():
-        dot_full(y_ref, first_ref, c_ref)
-        dot_full(s_ref, ct_ref, y_ref, d_ref)
-
-    hard = invert(s_ref, a_ref, x_ref, r_ref, t_ref, refresh, hard_ref[0] > 0)
-
+    hard = jnp.logical_or(near_inverse(s_ref, x_ref), hard_ref[0] > 0)
     leaving = pltpu.make_async_copy(z_ref, solved_ref, sem)
 
     def candidate_sum(terms):
@@ -281,8 +272,17 @@
         score_ref[...] = (gain - penalty) / (1.0 + gain)
         leaving.wait()
 
+    own, y = (own_ref[...],), split(y_ref[...])
+    left = other_ref[...].astype(F32) - dot_split(own, y)
+    z_other = dot_split(split(left), split(x_ref[...]))
+    z_own = dot_split(own, split(first_ref[...])) - dot_split(split(z_other), y, ((1,), (1,)))
+    outputs(z_own, z_other)
+
     @pl.when(hard)
     def _():
+        dot_full(y_ref, first_ref, c_ref)
+        dot_full(s_ref, ct_ref, y_ref, d_ref)
+        full_inverse(s_ref, x_ref, a_ref, r_ref, t_ref)
         count_rows = left_ref.shape[0]
         top, bottom = pl.ds(0, count_rows), pl.ds(count_rows, count_rows)
         z_own, z_other = a_ref.at[top], a_ref.at[bottom]
@@ -307,14 +307,6 @@
 
         lax.fori_loop(0, REFINEMENTS, refine, 0)
         outputs(z_own[...], z_other[...])
-
-    @pl.when(jnp.logical_not(hard))
-    def _():
-        own, y = (own_ref[...],), split(y_ref[...])
-        left = other_ref[...].astype(F32) - dot_split(own, y)
-        z_other = dot_split(split(left), split(x_ref[...]))
-        z_own = dot_split(own, split(first_ref[...])) - dot_split(split(z_other), y, ((1,), (1,)))
-        outputs(z_own, z_other)
 
 
 SMEM = pl.BlockSpec(memory_space=pltpu.SMEM)
@@ -343,9 +335,10 @@
 
 def from_others(array, axis):
     devices = lax.axis_size(axis)
+    shifts = sorted(range(1, devices), key=lambda shift: min(shift, devices - shift))
     return [
         lax.ppermute(array, axis, [(i, (i + shift) % devices) for i in range(devices)])
-        for shift in range(1, devices)
+        for shift in shifts
     ]
 
 
@@ -382,14 +375,15 @@
         pltpu.with_memory_space_constraint(labeled, pltpu.HBM),
         pltpu.with_memory_space_constraint(own, pltpu.HBM),
     )
+    damping_other = lax.ppermute(damping, "layer", swap)
+    other, damping_other = lax.optimization_barrier((other, damping_other))
     products = call(gram_kernel, slabs(rows), [SMEM] + [VMEM] * 4, 16, 500)(
         core, keep, own_t, own, other
     )
     sheet = exchanged(products, NEAR)
     partial = call(sum_kernel, slabs(rows // lax.axis_size(NEAR)), [VMEM], 8, 50)(sheet)
-    partial, damping = lax.optimization_barrier((partial, damping))
+    partial, damping_other = lax.optimization_barrier((partial, damping_other))
     partials = [partial, *from_others(partial, FAR)]
-    damping_other = lax.ppermute(damping, "layer", swap)
     damps = call(damp_kernel, slabs(16), [SMEM] * 2, 8, 50)(damping, damping_other)
     *partials, damps = lax.optimization_barrier((*partials, damps))
     total = call(total_kernel, slabs(rows), [VMEM] * planes, 8, 50)(*partials)

time: 253 us -> 274 us (1.083)
  Pallas kernels: 191 us -> 212 us
    pallas_call x1, Pallas kernels: 126 us -> 137 us  [on_device(): call(functools.partial(solve_kernel, count), (jax.ShapeDtypeStruct((row_c...]
    pallas_call x1, Pallas kernels: 62.7 us -> 71.8 us  [on_device(): call(functools.partial(first_kernel, count), (matrix, jax.ShapeDtypeStruc...]
  transfers between devices with their start and end apart: 6 -> 6, of which waited for: 4 -> 3; matrix products, arithmetic and copies ran while one was open for 0% -> 0% of each run, Pallas kernels for 25% -> 27%
where the time goes in v10:
time: 274 us; the launch traced here: 272 us
  Pallas kernels  212 us (77%)
  blocking collectives  46.6 us (17%)
  starting transfers between devices  9.89 us (4%)
    pallas_call x1, Pallas kernels, on_device(): call(functools.partial(solve_kernel, count), (jax.ShapeDtypeStruct((row_c...  137 us
    pallas_call x1, Pallas kernels, on_device(): call(functools.partial(first_kernel, count), (matrix, jax.ShapeDtypeStruc...  71.8 us
    all_to_all x2, blocking collectives, exchanged(): lax.all_to_all(array.reshape(devices, 1, -1), axis, 0, 0, tiled=True)  46.6 us
    ppermute x3, starting transfers between devices, from_others(): lax.ppermute(array, axis, [(i, (i + shift) % devices) for i in range(devi...  9.3 us
  transfers between devices with their start and end apart: 6, of which 3 were waited for; matrix products, arithmetic and copies ran while one was open for 0% of the time, Pallas kernels for 27%

profile of v10, /device:TPU:8, one launch (start us, length us, event | category | flops | bytes accessed | tf_op | source)
XLA Modules:
  0.0 272.2 jit_solution(16396327523995736372)
XLA Ops:
  0.6 0.1 collective-permute-start
  0.7 0.5 collective-permute-start.1
  1.2 1.1 shard_map.50
  2.3 0.1 collective-permute-done.1.damp_other_ref
  2.5 0.0 collective-permute-done.other_ref
  2.5 0.4 shard_map.51
  2.9 26.3 %all_to_all.10 = f32[32,1,8704]{2,1,0:T(1,128)S(1)} all-to-all(f32[32,1,8704]{2,1,0:T(1,128)S(1)} %bitcast.10), channel_id=1, replica_groups=mesh['layer'=2,'z_hi'=4,'z_lo'=2,'y'=4,'x'=4] {'z_lo','y','x'}, dimensions={0} | all-to-all | bytes 2228224 | tf_op jit(solution)/shard_map/all_to_all | solution.py:332
  29.2 0.1 shard_map.52.refs_0_
  29.2 6.4 %collective-permute-start.4 = (f32[68,128]{1,0:T(8,128)S(1)}, f32[68,128]{1,0:T(8,128)S(1)}, u32[]{:S(2)}, u32[]{:S(2)}) collective-permute-start(f32[68,128]{1,0:T(8,128)S(1)} %shard_map.52.refs_0_), channel_id=1, source_target_pairs={{0,64},{32,96},{64,0},{96,32},{1,65},{33,97},{65,1},{97,33},{2,66}... | collective-permute-start | bytes 104456 | tf_op jit(solution)/shard_map/ppermute | solution.py:340
  35.6 0.6 collective-permute-start.3
  36.2 2.4 collective-permute-start.2
  39.2 0.6 shard_map.53.damp_ref.damps_ref
  39.8 0.0 collective-permute-done.4.refs_3_
  39.8 0.8 collective-permute-done.3.refs_2_
  40.6 1.7 collective-permute-done.2.refs_1_
  42.3 0.1 shard_map.54
  42.4 20.3 %all_to_all.11 = f32[32,1,8704]{2,1,0:T(1,128)S(1)} all-to-all(f32[32,1,8704]{2,1,0:T(1,128)S(1)} %bitcast.9), channel_id=1, replica_groups=mesh['layer'=2,'z_hi'=4,'z_lo'=2,'y'=4,'x'=4] {'z_lo','y','x'}, dimensions={0} | all-to-all | bytes 2228224 | tf_op jit(solution)/shard_map/all_to_all | solution.py:332
  62.7 0.0 collective-permute-start.5
  62.7 71.8 %shard_map.55 = (f32[512,512]{1,0:T(8,128)S(1)}, s32[1]{0:T(128)}) custom-call(f32[16,128]{1,0:T(8,128)S(1)} %shard_map.53.damp_ref.damps_ref, f32[2176,128]{1,0:T(8,128)S(1)} %bitcast.13), custom_call_target="tpu_custom_call" | custom-call | flops 3000000000 | bytes 1048576 | tf_op jit(solution)/shard_map/pallas_call | solution.py:392
  134.5 0.0 collective-permute-done.5.theirs_ref
  134.6 137.5 %shard_map.56 = (f32[256,512]{1,0:T(8,128)}, f32[1,256]{1,0:T(1,128)}) custom-call(s32[1]{0:T(128)} %bitcast.core_ref, s32[1]{0:T(128)} %get-tuple-element.30.hard_ref, f32[16,128]{1,0:T(8,128)S(1)} %shard_map.53.damp_ref.damps_ref, f32[2176,128]{1,0:T(8,128)S(1)} %bitcast.14, f32[2176,128]{1,0:T(8,128)S(1)} %collective-permute-done.5.theirs_ref, ...), custom_call_target="tpu_custom_call" | custom-call | flops 6000000000 | bytes 1048576 | tf_op jit(solution)/shard_map/pallas_call | solution.py:401
Async XLA Ops:
  0.6 1.8 collective-permute-start
  0.7 1.7 collective-permute-start.1
  29.2 10.6 %collective-permute-start.4 = (f32[68,128]{1,0:T(8,128)S(1)}, f32[68,128]{1,0:T(8,128)S(1)}, u32[]{:S(2)}, u32[]{:S(2)}) collective-permute-start(f32[68,128]{1,0:T(8,128)S(1)} %shard_map.52.refs_0_), channel_id=1, source_target_pairs={{0,64},{32,96},{64,0},{96,32},{1,65},{33,97},{65,1},{97,33},{2,66}... | collective-permute-start | bytes 104456 | tf_op jit(solution)/shard_map/ppermute | solution.py:340
  35.6 5.0 %collective-permute-start.3 = (f32[68,128]{1,0:T(8,128)S(1)}, f32[68,128]{1,0:T(8,128)S(1)}, u32[]{:S(2)}, u32[]{:S(2)}) collective-permute-start(f32[68,128]{1,0:T(8,128)S(1)} %shard_map.52.refs_0_), channel_id=1, source_target_pairs={{0,96},{32,0},{64,32},{96,64},{1,97},{33,1},{65,33},{97,65},{2,98}... | collective-permute-start | bytes 104456 | tf_op jit(solution)/shard_map/ppermute | solution.py:340
  36.2 6.1 %collective-permute-start.2 = (f32[68,128]{1,0:T(8,128)S(1)}, f32[68,128]{1,0:T(8,128)S(1)}, u32[]{:S(2)}, u32[]{:S(2)}) collective-permute-start(f32[68,128]{1,0:T(8,128)S(1)} %shard_map.52.refs_0_), channel_id=1, source_target_pairs={{0,32},{32,64},{64,96},{96,0},{1,33},{33,65},{65,97},{97,1},{2,34}... | collective-permute-start | bytes 104456 | tf_op jit(solution)/shard_map/ppermute | solution.py:340
  62.7 71.8 %collective-permute-start.5 = (f32[2176,128]{1,0:T(8,128)S(1)}, f32[2176,128]{1,0:T(8,128)S(1)}, u32[]{:S(2)}, u32[]{:S(2)}) collective-permute-start(f32[2176,128]{1,0:T(8,128)S(1)} %bitcast.12), channel_id=1, source_target_pairs={{0,128},{128,0},{1,129},{129,1},{2,130},{130,2},{3,131},{131,3},{4... | collective-permute-start | bytes 3342344 | tf_op jit(solution)/shard_map/ppermute | solution.py:391
